TPU v7x, 32 devices: a whole 2x2x4 slice. The times are simulated.
32 devices in a mesh: dom: 8 (over z, y), ray: 4 (over x, core).
Axes of the slice: x: 2, y: 2, z: 4, core: 2. Of those that a mesh axis runs over, the one named last changes fastest.
Arguments:
- projections: bfloat16 [8, 64, 8192], P('dom', None, 'ray'), may hold values from -6 to 6
- phase_kernel: bfloat16 [129], replicated, may hold values from -0.5 to 0.5
- image: bfloat16 [16384, 64], P('dom'), may hold values from -6 to 6
- tile_library: bfloat16 [8, 4, 16, 128, 128], P('dom', 'ray'), may hold values from -0.09375 to 0.09375
- tile_entry: int32 [8, 4, 256], P('dom', 'ray'), may hold values from 0 to 15
- tile_image: int32 [8, 4, 256], P('dom', 'ray'), may hold values from 0 to 15
- tile_slot: int32 [8, 4, 256], P('dom', 'ray'), may hold values from 0 to 7
- tile_count: int32 [8, 4], P('dom', 'ray'), may hold values from 64 to 256, as said below
- slot_block: int32 [8, 4, 8], P('dom', 'ray'), may hold values from 0 to 15
Outputs:
- residual: bfloat16 [8, 64, 8192], P('dom', None, 'ray')
- image_next: float32 [16384, 64], P(('dom', 'ray'))
Inputs may be any that keep to these rules, and one draw needn't show every extreme that they name: `tile_count`: each device has at most 256 live tiles; some device holds exactly 256. Entries beyond a device's count are not used.
All inputs are finite; a program needn't handle non-finite values.
Results may differ from a plain program's by a relative error of at most 0.0075.
Values may be sent and summed in bfloat16 or wider, within the bound.
A program may use at most 64 MiB of HBM per device.

v0:
```python
import functools

import jax
import jax.numpy as jnp
from jax import lax
from jax.experimental import pallas as pl
from jax.experimental.pallas import tpu as pltpu
from jax.sharding import PartitionSpec as P

SMOOTH = 8


relax_factor = 0.25


def with_halo(cells, sides, width):
    for axis, dim in sides:
        count = lax.axis_size(axis)
        ends = count - 1
        head = lax.slice_in_dim(cells, 0, width, axis=dim)
        tail = lax.slice_in_dim(cells, cells.shape[dim] - width, cells.shape[dim], axis=dim)
        cells = jnp.concatenate(
            [
                lax.ppermute(tail, axis, [(i, (i + 1) % count) for i in range(ends)]),
                cells,
                lax.ppermute(head, axis, [((i + 1) % count, i) for i in range(ends)]),
            ],
            axis=dim,
        )
    return cells


def toeplitz(kernel, tile_size):
    taps = kernel.shape[0]
    padded = jnp.concatenate([kernel, jnp.zeros((2 * tile_size + 1 - taps,), kernel.dtype)])
    tiled = jnp.tile(padded, tile_size)[: 2 * tile_size * tile_size]
    return tiled.reshape(tile_size, 2 * tile_size).T


def phase_filter(projections, phase_kernel, tile_size):
    half_width = (phase_kernel.shape[0] - 1) // 2
    angles, slices, columns = projections.shape
    block_count = columns // tile_size
    rimmed = with_halo(projections, (("ray", 2),), half_width)
    padded = jnp.pad(rimmed, ((0, 0), (0, 0), (0, 2 * tile_size - 2 * half_width)))
    blocks = padded.reshape(angles, slices, block_count + 2, tile_size)
    windows = jnp.concatenate(
        [blocks[:, :, :block_count], blocks[:, :, 1 : block_count + 1]], axis=-1
    )
    filtered = jnp.einsum(
        "asbi,ij->asbj",
        windows,
        toeplitz(phase_kernel, tile_size),
        preferred_element_type=jnp.float32,
    )
    return filtered.reshape(angles, slices, columns).astype(jnp.bfloat16)


def stripe_profile(gathered):
    profile = jnp.median(gathered.astype(jnp.float32), axis=0)
    columns = profile.shape[1]
    rimmed = with_halo(profile, (("ray", 1),), SMOOTH)
    window_sum = jnp.zeros_like(profile)
    for offset in range(2 * SMOOTH + 1):
        window_sum = window_sum + rimmed[:, offset : offset + columns]
    position = lax.axis_index("ray") * columns + jnp.arange(columns)
    detector = lax.axis_size("ray") * columns
    in_range = (
        jnp.minimum(position + SMOOTH, detector - 1) - jnp.maximum(position - SMOOTH, 0) + 1
    ).astype(jnp.float32)
    return (profile - window_sum / in_range).astype(jnp.bfloat16)


def shards(
    projections,
    phase_kernel,
    image,
    tile_library,
    tile_entry,
    tile_image,
    tile_slot,
    tile_count,
    slot_block,
):
    tile_size = tile_library.shape[-1]
    angles, slices, columns = projections.shape
    phase = phase_filter(projections, phase_kernel, tile_size)
    gathered = lax.all_to_all(phase, "dom", split_axis=1, concat_axis=0, tiled=True)
    stripe = stripe_profile(gathered)
    fixed_rows = (gathered.astype(jnp.float32) - stripe.astype(jnp.float32)[None]).astype(
        jnp.bfloat16
    )
    corrected = lax.all_to_all(fixed_rows, "dom", split_axis=0, concat_axis=1, tiled=True)
    owners = lax.axis_size("dom")
    library = tile_library[0, 0]
    entries = tile_entry[0, 0]
    images = tile_image[0, 0]
    slots = tile_slot[0, 0]
    capacity = entries.shape[0]
    block_size = 64
    turn_count = capacity // block_size
    image_blocks = image.reshape(-1, tile_size, slices)
    block_total = image_blocks.shape[0]
    live_mask = jnp.arange(capacity) < tile_count[0, 0]
    slot_target = jnp.where(live_mask, slots, owners)
    image_target = jnp.where(live_mask, images, block_total)

    def forward_turn(turn_index, partial_value):
        first_tile = turn_index * block_size
        chosen = lax.dynamic_slice_in_dim(entries, first_tile, block_size)
        placed = lax.dynamic_slice_in_dim(images, first_tile, block_size)
        destined = lax.dynamic_slice_in_dim(slot_target, first_tile, block_size)
        product = jnp.einsum(
            "krp,kps->ksr",
            library[chosen],
            image_blocks[placed],
            preferred_element_type=jnp.float32,
        )
        return partial_value.at[destined].add(product, mode="drop")

    partial_value = lax.fori_loop(
        0, turn_count, forward_turn, jnp.zeros((owners, slices, tile_size), jnp.float32)
    )
    received = lax.all_to_all(
        partial_value.astype(jnp.bfloat16), "dom", split_axis=0, concat_axis=0, tiled=True
    )
    per_owner = columns // tile_size
    carried = slot_block[0, 0]
    block_ids = jnp.arange(angles * per_owner).reshape(angles, per_owner)
    selector = (block_ids[:, :, None] == carried[None, None, :]).astype(jnp.bfloat16)
    forward = jnp.einsum("abd,dst->asbt", selector, received, preferred_element_type=jnp.float32)
    residual = (corrected.astype(jnp.float32) - forward.reshape(angles, slices, columns)).astype(
        jnp.bfloat16
    )
    back = jnp.einsum(
        "abd,asbt->dst",
        selector,
        residual.reshape(angles, slices, per_owner, tile_size),
        preferred_element_type=jnp.float32,
    ).astype(jnp.bfloat16)
    returned = lax.all_to_all(back, "dom", split_axis=0, concat_axis=0, tiled=True)

    def adjoint_turn(turn_index, gradient):
        first_tile = turn_index * block_size
        chosen = lax.dynamic_slice_in_dim(entries, first_tile, block_size)
        sourced = lax.dynamic_slice_in_dim(slots, first_tile, block_size)
        destined = lax.dynamic_slice_in_dim(image_target, first_tile, block_size)
        product = jnp.einsum(
            "krp,ksr->kps", library[chosen], returned[sourced], preferred_element_type=jnp.float32
        )
        return gradient.at[destined].add(product, mode="drop")

    gradient = lax.fori_loop(
        0, turn_count, adjoint_turn, jnp.zeros((block_total, tile_size, slices), jnp.float32)
    )
    gradient = gradient.reshape(-1, slices)
    rows_own = gradient.shape[0] // lax.axis_size("ray")
    update = lax.psum_scatter(gradient, "ray", scatter_dimension=0, tiled=True)
    own_image = lax.dynamic_slice_in_dim(image, lax.axis_index("ray") * rows_own, rows_own)
    image_next = own_image.astype(jnp.float32) + relax_factor * update
    return (residual, image_next)


MESH = pl.DeviceIdType.MESH
NT = (((1,), (1,)), ((), ()))
NN = (((1,), (0,)), ((), ()))


def dot(a, b, dims):
    return lax.dot_general(a, b, dims, preferred_element_type=jnp.float32)


def sort_pairs(count):
    p = 1
    while p < count:
        k = p
        while k >= 1:
            for j in range(k % p, count - k, 2 * k):
                for i in range(min(k, count - j - k)):
                    if (i + j) // (2 * p) == (i + j + k) // (2 * p):
                        yield i + j, i + j + k
            k //= 2
        p *= 2


def step_kernel(
    owners,
    quarters,
    taps_ref,
    proj_any,
    image_any,
    library_any,
    entry_ref,
    place_ref,
    slot_ref,
    count_ref,
    carried_ref,
    residual_ref,
    next_ref,
    rim,
    phase_out,
    phase_in,
    shifted,
    mixed,
    partial_rows,
    partial_out,
    partial_in,
    stripes,
    forward,
    blocks,
    back_out,
    back_in,
    back_rows,
    update_rows,
    update_out,
    update_in,
    halo_send,
    halo_recv,
    phase_send,
    phase_recv,
    stripe_send,
    stripe_recv,
    partial_send,
    partial_recv,
    back_send,
    back_recv,
    update_send,
    update_recv,
    taps_wide,
    proj_ref,
    image_rows,
    image_ref,
    library_ref,
    load_sem,
):
    f32, bf16 = jnp.float32, jnp.bfloat16
    me, ray = lax.axis_index("dom"), lax.axis_index("ray")
    slices, columns = proj_ref.shape
    tile = library_ref.shape[-1]
    entries = library_ref.shape[0]
    places = image_rows.shape[0] // tile
    count = columns // tile
    per = slices // owners
    half = tile // 2
    own_places = places // quarters

    def dom_peer(k):
        return lax.rem(me + k, owners)

    def ray_peer(k):
        return lax.rem(ray + k, quarters)

    loads = [
        pltpu.make_async_copy(proj_any.at[0], proj_ref, load_sem.at[0]),
        pltpu.make_async_copy(image_any, image_rows, load_sem.at[1]),
        pltpu.make_async_copy(library_any.at[0, 0], library_ref, load_sem.at[2]),
    ]
    for copy in loads:
        copy.start()

    barrier = pltpu.get_barrier_semaphore()
    for k in range(1, owners):
        pl.semaphore_signal(barrier, inc=1, device_id=(dom_peer(k), ray), device_id_type=MESH)
    for k in range(1, quarters):
        pl.semaphore_signal(barrier, inc=1, device_id=(me, ray_peer(k)), device_id_type=MESH)

    def dom_copy(src, dst, send, recv, k):
        return pltpu.make_async_remote_copy(
            src_ref=src,
            dst_ref=dst,
            send_sem=send.at[k],
            recv_sem=recv.at[k],
            device_id=(dom_peer(k), ray),
            device_id_type=MESH,
        )

    def ray_copy(src, dst, send, recv, slot, k):
        return pltpu.make_async_remote_copy(
            src_ref=src,
            dst_ref=dst,
            send_sem=send.at[slot],
            recv_sem=recv.at[slot],
            device_id=(me, ray_peer(k)),
            device_id_type=MESH,
        )

    taps_wide[...] = jnp.zeros((1, 2 * tile), f32)
    taps_wide[:, : taps_ref.shape[1]] = taps_ref[...].astype(f32)
    spread = jnp.broadcast_to(taps_wide[...], (tile, 2 * tile))
    weights = pltpu.roll(spread, 0, 1, stride=1, stride_axis=0).astype(bf16)

    loads[0].wait()
    pl.semaphore_wait(barrier, owners + quarters - 2)

    halos = [
        ray_copy(
            proj_ref.at[:, pl.ds(columns - tile, tile)], rim.at[0], halo_send, halo_recv, 0, 1
        ),
        ray_copy(
            proj_ref.at[:, pl.ds(0, tile)],
            rim.at[count + 1],
            halo_send,
            halo_recv,
            1,
            quarters - 1,
        ),
    ]
    for copy in halos:
        copy.start()

    capacity = entry_ref.shape[1]
    slot = slot_ref[...]
    relative = jnp.where(slot >= me, slot - me, slot - me + owners)
    alive = lax.broadcasted_iota(jnp.int32, (1, capacity), 1) < count_ref[0, 0]
    code = jnp.where(alive, entry_ref[...] * owners + relative, -1)
    pick = jnp.where(
        lax.broadcasted_iota(jnp.int32, (entries * owners, capacity), 0) == code, 1.0, 0.0
    ).astype(bf16)
    where_to = jnp.where(
        lax.broadcasted_iota(jnp.int32, (places, capacity), 0) == place_ref[...], 1.0, 0.0
    ).astype(bf16)
    uses = dot(pick, where_to, NT).astype(bf16)
    uses_back = dot(where_to, pick, NT).astype(bf16)

    for b in range(count):
        rim[b + 1] = proj_ref[:, b * tile : (b + 1) * tile]
    loads[1].wait()
    for place in range(places):
        image_ref[pl.ds(place, slices, stride=places), :] = (
            image_rows[place * tile : (place + 1) * tile, :].astype(f32).T
        )

    group = 8

    def mix(step, carry):
        for inner in range(group):
            s = step * group + inner
            start = pl.multiple_of(s * places, places)
            piece = image_ref[pl.ds(start, places), :].astype(bf16)
            mixed[s] = dot(uses, piece, NN).reshape(entries, owners, tile)
        return carry

    lax.fori_loop(0, slices // group, mix, 0)

    loads[2].wait()
    total = jnp.zeros((slices * owners, tile), f32)
    for entry in range(0, entries, 2):
        left = jnp.concatenate(
            [
                mixed[:, entry].reshape(slices * owners, tile).astype(bf16),
                mixed[:, entry + 1].reshape(slices * owners, tile).astype(bf16),
            ],
            axis=1,
        )
        right = jnp.concatenate([library_ref[entry], library_ref[entry + 1]], axis=1)
        total = total + dot(left, right, NT)
    partial_rows[...] = total
    for k in range(1, owners):
        partial_out[k] = partial_rows[pl.ds(k, slices, stride=owners), :].astype(bf16)
    partial_in[me] = partial_rows[pl.ds(0, slices, stride=owners), :].astype(bf16)
    partials = [
        dom_copy(partial_out.at[k], partial_in.at[me], partial_send, partial_recv, k)
        for k in range(1, owners)
    ]
    for copy in partials:
        copy.start()

    for copy in halos:
        copy.wait()

    @pl.when(ray == 0)
    def _():
        rim[0] = jnp.zeros((slices, tile), bf16)

    @pl.when(ray == quarters - 1)
    def _():
        rim[count + 1] = jnp.zeros((slices, tile), bf16)

    rows = (count + 1) * slices
    phase = dot(rim[0 : count + 1].reshape(rows, tile), weights[:, :tile], NT)
    phase = phase + dot(rim[1 : count + 2].reshape(rows, tile), weights[:, tile:], NT)
    phase = phase.astype(bf16).astype(f32)
    grouped = phase.reshape(count + 1, owners, per, tile)
    for owner in range(owners):
        phase_out[owner] = grouped[:, owner].astype(bf16)
    phase_in[0] = phase_out[me]
    phases = [
        dom_copy(phase_out.at[dom_peer(k)], phase_in.at[k], phase_send, phase_recv, k)
        for k in range(1, owners)
    ]
    for copy in phases:
        copy.start()

    turned = pltpu.roll(phase, half, 1).reshape(count + 1, slices, tile)
    lane = lax.broadcasted_iota(jnp.int32, (1, 1, tile), 2)
    shifted[...] = jnp.where(lane < half, turned[:count], turned[1:])

    for copy in phases:
        copy.wait_recv()

    values = [phase_in[a].astype(f32) for a in range(owners)]
    for i, j in sort_pairs(owners):
        values[i], values[j] = jnp.minimum(values[i], values[j]), jnp.maximum(values[i], values[j])
    middle = (values[owners // 2 - 1] + values[owners // 2]) * 0.5
    profile = jnp.concatenate([middle[b] for b in range(count + 1)], axis=1)
    width = columns + tile
    detector = quarters * columns
    position = ray * columns - half + lax.broadcasted_iota(jnp.int32, (1, width), 1)
    profile = jnp.where((position >= 0) & (position < detector), profile, 0.0)
    run = profile
    reach = 1
    while reach < 2 * SMOOTH:
        run = run + pltpu.roll(run, reach, 1)
        reach *= 2
    window = pltpu.roll(run, width - (SMOOTH - 1), 1) + pltpu.roll(profile, width - SMOOTH, 1)
    in_range = (
        jnp.minimum(position + SMOOTH, detector - 1) - jnp.maximum(position - SMOOTH, 0) + 1
    ).astype(f32)
    stripe = pltpu.roll(profile - window / in_range, width - half, 1)
    for b in range(count):
        stripes[me, b] = stripe[:, b * tile : (b + 1) * tile].astype(bf16)
    steps = owners // 2
    beside = 1 - 2 * lax.rem(me, 2)

    def stripe_copy(source, k, slot):
        return pltpu.make_async_remote_copy(
            src_ref=stripes.at[source],
            dst_ref=stripes.at[source],
            send_sem=stripe_send.at[slot],
            recv_sem=stripe_recv.at[slot],
            device_id=(lax.rem(me + k + owners, owners), ray),
            device_id_type=MESH,
        )

    spreads = [stripe_copy(me, 2 * k, k) for k in range(1, steps)]
    spreads = spreads + [stripe_copy(me, beside, 0)]
    for copy in spreads:
        copy.start()

    for copy in partials:
        copy.wait_recv()

    def project(b, carry):
        total = jnp.zeros((slices, tile), f32)
        for d in range(owners):
            share = jnp.where(carried_ref[0, d] == b, 1.0, 0.0).astype(f32)
            total = total + share * partial_in[d].astype(f32)
        forward[b] = total
        return carry

    lax.fori_loop(0, count, project, 0)

    spreads[-1].wait_recv()
    relays = []
    for k in range(1, steps):
        spreads[k - 1].wait_recv()
        relays.append(stripe_copy(lax.rem(me - 2 * k + owners, owners), beside, steps + k))
        relays[-1].start()
    for copy in relays:
        copy.wait_recv()

    for b in range(count):
        stripe_all = jnp.concatenate([stripes[o, b].astype(f32) for o in range(owners)], axis=0)
        corrected = (shifted[b] - stripe_all).astype(bf16).astype(f32)
        rest = (corrected - forward[b]).astype(bf16)
        blocks[b] = rest
        residual_ref[:, b * tile : (b + 1) * tile] = rest

    for k in range(1, owners):
        back_out[k] = blocks[carried_ref[0, dom_peer(k)]]
    backs = [
        dom_copy(back_out.at[k], back_in.at[owners - k], back_send, back_recv, k)
        for k in range(1, owners)
    ]
    for copy in backs:
        copy.start()
    back_in[0] = blocks[carried_ref[0, me]]
    for copy in backs:
        copy.wait_recv()

    for k in range(owners):
        back_rows[pl.ds(k, slices, stride=owners), :] = back_in[k].astype(f32)
    parts = update_out.shape[0]
    part = slices // parts
    updates = []
    for turn in range(parts):
        rows = part * owners
        gathered = back_rows[turn * rows : (turn + 1) * rows, :].astype(bf16)
        first = turn * part
        for entry in range(entries):
            mixed[first : first + part, entry] = dot(gathered, library_ref[entry], NN).reshape(
                part, owners, tile
            )

        def unmix(step, carry, first=first):
            for inner in range(group):
                s = first + step * group + inner
                piece = mixed[s].reshape(entries * owners, tile).astype(bf16)
                start = pl.multiple_of(s * places, places)
                update_rows[pl.ds(start, places), :] = dot(uses_back, piece, NN)
            return carry

        lax.fori_loop(0, part // group, unmix, 0)
        for place in range(places):
            update_out[turn, place // own_places, place % own_places] = update_rows[
                pl.ds(first * places + place, part, stride=places), :
            ].astype(bf16)
        sent = [
            ray_copy(
                update_out.at[turn, ray_peer(k)],
                update_in.at[turn, k],
                update_send,
                update_recv,
                turn * quarters + k,
                k,
            )
            for k in range(1, quarters)
        ]
        for copy in sent:
            copy.start()
        updates = updates + sent
    for copy in updates:
        copy.wait_recv()
    for place in range(own_places):
        amounts = []
        for turn in range(parts):
            amount = update_out[turn, ray, place].astype(f32)
            for k in range(1, quarters):
                amount = amount + update_in[turn, k, place].astype(f32)
            amounts.append(amount)
        update = jnp.concatenate(amounts, axis=0).T
        start = pl.multiple_of((ray * own_places + place) * tile, tile)
        held = image_rows[pl.ds(start, tile), :].astype(f32)
        next_ref[place * tile : (place + 1) * tile, :] = held + relax_factor * update
    for copy in phases + partials + spreads + relays + backs + updates:
        copy.wait_send()


def fast_shards(
    projections,
    phase_kernel,
    image,
    tile_library,
    tile_entry,
    tile_image,
    tile_slot,
    tile_count,
    slot_block,
):
    f32, bf16 = jnp.float32, jnp.bfloat16
    owners, quarters = lax.axis_size("dom"), lax.axis_size("ray")
    entries, tile = tile_library.shape[2], tile_library.shape[-1]
    _, slices, columns = projections.shape
    count = columns // tile
    places = image.shape[0] // tile
    per = slices // owners
    own_places = places // quarters
    parts = 2
    hbm = pl.BlockSpec(memory_space=pl.ANY)
    vmem = pl.BlockSpec(memory_space=pltpu.VMEM)
    smem = pl.BlockSpec(memory_space=pltpu.SMEM)
    sems = pltpu.SemaphoreType.DMA
    residual, image_next = pl.pallas_call(
        functools.partial(step_kernel, owners, quarters),
        out_shape=(
            jax.ShapeDtypeStruct((slices, columns), bf16),
            jax.ShapeDtypeStruct((own_places * tile, slices), f32),
        ),
        in_specs=[vmem] + [hbm] * 3 + [vmem] * 3 + [smem] * 2,
        out_specs=(vmem, vmem),
        scratch_shapes=[
            pltpu.VMEM((count + 2, slices, tile), bf16),
            pltpu.VMEM((owners, count + 1, per, tile), bf16),
            pltpu.VMEM((owners, count + 1, per, tile), bf16),
            pltpu.VMEM((count, slices, tile), f32),
            pltpu.VMEM((slices, entries, owners, tile), f32),
            pltpu.VMEM((slices * owners, tile), f32),
            pltpu.VMEM((owners, slices, tile), bf16),
            pltpu.VMEM((owners, slices, tile), bf16),
            pltpu.VMEM((owners, count, per, tile), bf16),
            pltpu.VMEM((count, slices, tile), f32),
            pltpu.VMEM((count, slices, tile), bf16),
            pltpu.VMEM((owners, slices, tile), bf16),
            pltpu.VMEM((owners, slices, tile), bf16),
            pltpu.VMEM((slices * owners, tile), f32),
            pltpu.VMEM((slices * places, tile), f32),
            pltpu.VMEM((parts, quarters, own_places, slices // parts, tile), bf16),
            pltpu.VMEM((parts, quarters, own_places, slices // parts, tile), bf16),
            sems((2,)),
            sems((2,)),
            sems((owners,)),
            sems((owners,)),
            sems((owners,)),
            sems((owners,)),
            sems((owners,)),
            sems((owners,)),
            sems((owners,)),
            sems((owners,)),
            sems((parts * quarters,)),
            sems((parts * quarters,)),
            pltpu.VMEM((1, 2 * tile), f32),
            pltpu.VMEM((slices, columns), bf16),
            pltpu.VMEM(image.shape, bf16),
            pltpu.VMEM((slices * places, tile), f32),
            pltpu.VMEM((entries, tile, tile), bf16),
            sems((3,)),
        ],
        compiler_params=pltpu.CompilerParams(
            collective_id=0, has_side_effects=True, vmem_limit_bytes=48 * 1024 * 1024
        ),
    )(
        phase_kernel[None],
        projections,
        image,
        tile_library,
        tile_entry[0],
        tile_image[0],
        tile_slot[0],
        tile_count,
        slot_block[0],
    )
    return residual[None], image_next


def fits_kernel(projections, phase_kernel, image, tile_library, tile_entry, *rest):
    owners, quarters = lax.axis_size("dom"), lax.axis_size("ray")
    tile = tile_library.shape[-1]
    angles, slices, columns = projections.shape
    return (
        angles == 1
        and slices % 16 == 0
        and slices == 8 * owners
        and owners == 8
        and tile == 128
        and phase_kernel.shape[0] == tile + 1
        and columns % tile == 0
        and tile_library.shape[2] % 2 == 0
        and (image.shape[0] // tile) % (16 * 1) == 0
        and (image.shape[0] // tile) % quarters == 0
        and tile_entry.shape[2] <= 256
    )


def any_shards(*args):
    if fits_kernel(*args):
        return fast_shards(*args)
    return shards(*args)


def solution(mesh):
    return jax.shard_map(
        any_shards,
        mesh=mesh,
        in_specs=(
            P("dom", None, "ray"),
            P(),
            P("dom", None),
            P("dom", "ray", None, None, None),
            P("dom", "ray", None),
            P("dom", "ray", None),
            P("dom", "ray", None),
            P("dom", "ray"),
            P("dom", "ray", None),
        ),
        out_specs=(P("dom", None, "ray"), P(("dom", "ray"), None)),
        check_vma=False,
    )
```

profile of v0, /device:TPU:0, one launch (start us, length us, event | category | flops | bytes accessed | tf_op | source)
XLA Modules:
  0.0 44.0 jit_solution(9278697744062260642)
XLA Ops:
  0.6 0.0 copy-start
  1.3 0.7 %broadcast_in_dim.6.taps_ref = bf16[1,129]{1,0:T(2,128)(2,1)S(1)} reshape(bf16[129]{0:T(256)(128)(2,1)} %param.10) | data formatting | bytes 516 | tf_op jit(solution)/shard_map/broadcast_in_dim | solution.py:612
  2.0 0.0 copy-start.1
  2.0 0.0 copy-start.2
  2.0 0.0 copy-start.3
  2.0 0.0 copy-start.4
  2.0 0.0 copy-start.5
  2.0 1.3 %copy.11.image_any = bf16[2048,64]{1,0:T(8,128)(2,1)S(1)} copy(bf16[2048,64]{0,1:T(8,128)(2,1)} %param.11) | data formatting | bytes 524288 | tf_op args[2]
  3.3 0.0 copy-done
  3.3 0.0 copy-done.1
  3.3 0.0 copy-done.2
  3.3 0.0 copy-done.3
  3.3 0.0 copy-done.4
  3.3 0.0 copy-done.5
  3.4 39.2 %shard_map.104 = (bf16[64,2048]{1,0:T(8,128)(2,1)S(1)}, f32[512,64]{1,0:T(8,128)S(1)}) custom-call(bf16[1,129]{1,0:T(2,128)(2,1)S(1)} %broadcast_in_dim.6.taps_ref, bf16[1,64,2048]{2,1,0:T(8,128)(2,1)S(1)} %copy-done.1, bf16[2048,64]{1,0:T(8,128)(2,1)S(1)} %copy.11.image_any, bf16[1,1,16,128,128]{4,3,2,1,0:T(8,128)(2,1)S(1)} %copy-done, ...), custom_call_target="tpu_custom_call" | custom-call | tf_op jit(solution)/shard_map/pallas_call | solution.py:563
  42.5 0.8 %copy.12 = f32[512,64]{0,1:T(8,128)} copy(f32[512,64]{1,0:T(8,128)S(1)} %get-tuple-element.7) | data formatting | bytes 262144
  43.3 0.7 %copy.15 = bf16[1,64,2048]{2,1,0:T(8,128)(2,1)} copy(bf16[1,64,2048]{2,1,0:T(8,128)(2,1)S(1)} %bitcast.5) | data formatting | bytes 524288
Async XLA Ops:
  0.6 2.7 %copy-start = (bf16[1,1,16,128,128]{4,3,2,1,0:T(8,128)(2,1)S(1)}, bf16[1,1,16,128,128]{4,3,2,1,0:T(8,128)(2,1)}, u32[]{:S(2)}) copy-start(bf16[1,1,16,128,128]{4,3,2,1,0:T(8,128)(2,1)} %library_any.1) | copy-start | bytes 1572868
  2.0 1.3 %copy-start.1 = (bf16[1,64,2048]{2,1,0:T(8,128)(2,1)S(1)}, bf16[1,64,2048]{2,1,0:T(8,128)(2,1)}, u32[]{:S(2)}) copy-start(bf16[1,64,2048]{2,1,0:T(8,128)(2,1)} %proj_any.1) | copy-start | bytes 786436
  2.0 1.3 %copy-start.2 = (s32[1,1,256]{2,1,0:T(1,128)S(1)}, s32[1,1,256]{2,1,0:T(1,128)}, u32[]{:S(2)}) copy-start(s32[1,1,256]{2,1,0:T(1,128)} %param.13) | copy-start | bytes 3076
  2.0 1.3 %copy-start.3 = (s32[1,1,256]{2,1,0:T(1,128)S(1)}, s32[1,1,256]{2,1,0:T(1,128)}, u32[]{:S(2)}) copy-start(s32[1,1,256]{2,1,0:T(1,128)} %param.14) | copy-start | bytes 3076
  2.0 1.3 %copy-start.4 = (s32[1,1,256]{2,1,0:T(1,128)S(1)}, s32[1,1,256]{2,1,0:T(1,128)}, u32[]{:S(2)}) copy-start(s32[1,1,256]{2,1,0:T(1,128)} %param.15) | copy-start | bytes 3076
  2.0 1.3 %copy-start.5 = (s32[1,1,8]{2,1,0:T(1,128)S(1)}, s32[1,1,8]{2,1,0:T(1,128)}, u32[]{:S(2)}) copy-start(s32[1,1,8]{2,1,0:T(1,128)} %param.17) | copy-start | bytes 100
where the time goes:
time: 44.2 us; the launch traced here: 44 us
  Pallas kernels  39.2 us (89%)
  local copies, waits for them, and re-layouts  3.42 us (8%)
  between operations  1.42 us (3%)
    pallas_call x1, Pallas kernels, fast_shards(): pl.pallas_call(functools.partial(step_kernel, owners, quarters), out_shap...  39.2 us
    unnamed x15, local copies, waits for them, and re-layouts  2.76 us

commit v1 on v0

v1 whole, which is shorter than its diff:
```python
import functools

import jax
import jax.numpy as jnp
from jax import lax
from jax.experimental import pallas as pl
from jax.experimental.pallas import tpu as pltpu
from jax.sharding import PartitionSpec as P

SMOOTH = 8


relax_factor = 0.25


def with_halo(cells, sides, width):
    for axis, dim in sides:
        count = lax.axis_size(axis)
        ends = count - 1
        head = lax.slice_in_dim(cells, 0, width, axis=dim)
        tail = lax.slice_in_dim(cells, cells.shape[dim] - width, cells.shape[dim], axis=dim)
        cells = jnp.concatenate(
            [
                lax.ppermute(tail, axis, [(i, (i + 1) % count) for i in range(ends)]),
                cells,
                lax.ppermute(head, axis, [((i + 1) % count, i) for i in range(ends)]),
            ],
            axis=dim,
        )
    return cells


def toeplitz(kernel, tile_size):
    taps = kernel.shape[0]
    padded = jnp.concatenate([kernel, jnp.zeros((2 * tile_size + 1 - taps,), kernel.dtype)])
    tiled = jnp.tile(padded, tile_size)[: 2 * tile_size * tile_size]
    return tiled.reshape(tile_size, 2 * tile_size).T


def phase_filter(projections, phase_kernel, tile_size):
    half_width = (phase_kernel.shape[0] - 1) // 2
    angles, slices, columns = projections.shape
    block_count = columns // tile_size
    rimmed = with_halo(projections, (("ray", 2),), half_width)
    padded = jnp.pad(rimmed, ((0, 0), (0, 0), (0, 2 * tile_size - 2 * half_width)))
    blocks = padded.reshape(angles, slices, block_count + 2, tile_size)
    windows = jnp.concatenate(
        [blocks[:, :, :block_count], blocks[:, :, 1 : block_count + 1]], axis=-1
    )
    filtered = jnp.einsum(
        "asbi,ij->asbj",
        windows,
        toeplitz(phase_kernel, tile_size),
        preferred_element_type=jnp.float32,
    )
    return filtered.reshape(angles, slices, columns).astype(jnp.bfloat16)


def stripe_profile(gathered):
    profile = jnp.median(gathered.astype(jnp.float32), axis=0)
    columns = profile.shape[1]
    rimmed = with_halo(profile, (("ray", 1),), SMOOTH)
    window_sum = jnp.zeros_like(profile)
    for offset in range(2 * SMOOTH + 1):
        window_sum = window_sum + rimmed[:, offset : offset + columns]
    position = lax.axis_index("ray") * columns + jnp.arange(columns)
    detector = lax.axis_size("ray") * columns
    in_range = (
        jnp.minimum(position + SMOOTH, detector - 1) - jnp.maximum(position - SMOOTH, 0) + 1
    ).astype(jnp.float32)
    return (profile - window_sum / in_range).astype(jnp.bfloat16)


def shards(
    projections,
    phase_kernel,
    image,
    tile_library,
    tile_entry,
    tile_image,
    tile_slot,
    tile_count,
    slot_block,
):
    tile_size = tile_library.shape[-1]
    angles, slices, columns = projections.shape
    phase = phase_filter(projections, phase_kernel, tile_size)
    gathered = lax.all_to_all(phase, "dom", split_axis=1, concat_axis=0, tiled=True)
    stripe = stripe_profile(gathered)
    fixed_rows = (gathered.astype(jnp.float32) - stripe.astype(jnp.float32)[None]).astype(
        jnp.bfloat16
    )
    corrected = lax.all_to_all(fixed_rows, "dom", split_axis=0, concat_axis=1, tiled=True)
    owners = lax.axis_size("dom")
    library = tile_library[0, 0]
    entries = tile_entry[0, 0]
    images = tile_image[0, 0]
    slots = tile_slot[0, 0]
    capacity = entries.shape[0]
    block_size = 64
    turn_count = capacity // block_size
    image_blocks = image.reshape(-1, tile_size, slices)
    block_total = image_blocks.shape[0]
    live_mask = jnp.arange(capacity) < tile_count[0, 0]
    slot_target = jnp.where(live_mask, slots, owners)
    image_target = jnp.where(live_mask, images, block_total)

    def forward_turn(turn_index, partial_value):
        first_tile = turn_index * block_size
        chosen = lax.dynamic_slice_in_dim(entries, first_tile, block_size)
        placed = lax.dynamic_slice_in_dim(images, first_tile, block_size)
        destined = lax.dynamic_slice_in_dim(slot_target, first_tile, block_size)
        product = jnp.einsum(
            "krp,kps->ksr",
            library[chosen],
            image_blocks[placed],
            preferred_element_type=jnp.float32,
        )
        return partial_value.at[destined].add(product, mode="drop")

    partial_value = lax.fori_loop(
        0, turn_count, forward_turn, jnp.zeros((owners, slices, tile_size), jnp.float32)
    )
    received = lax.all_to_all(
        partial_value.astype(jnp.bfloat16), "dom", split_axis=0, concat_axis=0, tiled=True
    )
    per_owner = columns // tile_size
    carried = slot_block[0, 0]
    block_ids = jnp.arange(angles * per_owner).reshape(angles, per_owner)
    selector = (block_ids[:, :, None] == carried[None, None, :]).astype(jnp.bfloat16)
    forward = jnp.einsum("abd,dst->asbt", selector, received, preferred_element_type=jnp.float32)
    residual = (corrected.astype(jnp.float32) - forward.reshape(angles, slices, columns)).astype(
        jnp.bfloat16
    )
    back = jnp.einsum(
        "abd,asbt->dst",
        selector,
        residual.reshape(angles, slices, per_owner, tile_size),
        preferred_element_type=jnp.float32,
    ).astype(jnp.bfloat16)
    returned = lax.all_to_all(back, "dom", split_axis=0, concat_axis=0, tiled=True)

    def adjoint_turn(turn_index, gradient):
        first_tile = turn_index * block_size
        chosen = lax.dynamic_slice_in_dim(entries, first_tile, block_size)
        sourced = lax.dynamic_slice_in_dim(slots, first_tile, block_size)
        destined = lax.dynamic_slice_in_dim(image_target, first_tile, block_size)
        product = jnp.einsum(
            "krp,ksr->kps", library[chosen], returned[sourced], preferred_element_type=jnp.float32
        )
        return gradient.at[destined].add(product, mode="drop")

    gradient = lax.fori_loop(
        0, turn_count, adjoint_turn, jnp.zeros((block_total, tile_size, slices), jnp.float32)
    )
    gradient = gradient.reshape(-1, slices)
    rows_own = gradient.shape[0] // lax.axis_size("ray")
    update = lax.psum_scatter(gradient, "ray", scatter_dimension=0, tiled=True)
    own_image = lax.dynamic_slice_in_dim(image, lax.axis_index("ray") * rows_own, rows_own)
    image_next = own_image.astype(jnp.float32) + relax_factor * update
    return (residual, image_next)


MESH = pl.DeviceIdType.MESH
NT = (((1,), (1,)), ((), ()))
NN = (((1,), (0,)), ((), ()))
SUB = 16


def dot(a, b, dims):
    return lax.dot_general(a, b, dims, preferred_element_type=jnp.float32)


def ordered(a, b):
    return jnp.minimum(a, b), jnp.maximum(a, b)


def sorted_four(a, b, c, d):
    a, b = ordered(a, b)
    c, d = ordered(c, d)
    a, c = ordered(a, c)
    b, d = ordered(b, d)
    b, c = ordered(b, c)
    return a, b, c, d


def median_of_eight(values):
    low = sorted_four(*values[:4])
    high = sorted_four(*values[4:])
    below = [jnp.minimum(low[i], high[3 - i]) for i in range(4)]
    above = [jnp.maximum(low[i], high[3 - i]) for i in range(4)]
    fourth = jnp.maximum(jnp.maximum(below[0], below[1]), jnp.maximum(below[2], below[3]))
    fifth = jnp.minimum(jnp.minimum(above[0], above[1]), jnp.minimum(above[2], above[3]))
    return (fourth + fifth) * 0.5


def step_kernel(
    owners,
    quarters,
    taps_any,
    proj_any,
    image_any,
    library_any,
    entry_any,
    place_any,
    slot_any,
    count_any,
    carried_any,
    residual_ref,
    next_ref,
    taps_ref,
    proj_ref,
    image_ref,
    library_ref,
    entry_ref,
    place_ref,
    slot_ref,
    count_ref,
    carried_own,
    carried_all,
    carried_ref,
    taps_wide,
    rim,
    phase_out,
    phase_in,
    profile_ref,
    fixed,
    counted,
    spread_ref,
    matrix,
    partial_out,
    partial_in,
    same_ref,
    back_out,
    back_in,
    rest_out,
    rest_in,
    own_update,
    update_out,
    update_in,
    load_sem,
    halo_send,
    halo_recv,
    carried_send,
    carried_recv,
    phase_send,
    phase_recv,
    edge_send,
    edge_recv,
    partial_send,
    partial_recv,
    back_send,
    back_recv,
    rest_send,
    rest_recv,
    update_send,
    update_recv,
):
    f32, bf16 = jnp.float32, jnp.bfloat16
    me, ray = lax.axis_index("dom"), lax.axis_index("ray")
    slices, columns = proj_ref.shape
    entries, tile = library_ref.shape[0], library_ref.shape[-1]
    places = image_ref.shape[1] // tile
    count = columns // tile
    ring = count + 1
    inner = count - 2
    per = slices // owners
    side = owners // 2
    half = tile // 2
    share = places * tile // quarters
    rows_half = side * per

    group, spot = me // side, lax.rem(me, side)

    def dom_peer(k):
        if k >= side:
            return (1 - group) * side + lax.rem(spot + k - side, side)
        return group * side + lax.rem(spot + k, side)

    dom_order = list(range(side, owners)) + list(range(1, side))

    chip, core = ray // 2, lax.rem(ray, 2)

    def ray_twin(k):
        chip_to = 1 - chip if k >= 2 else chip
        core_to = 1 - core if k % 2 else core
        return chip_to * 2 + core_to

    def ray_next(k):
        return lax.rem(ray + k, quarters)

    barrier = pltpu.get_barrier_semaphore()
    for k in range(1, owners):
        pl.semaphore_signal(barrier, inc=1, device_id=(dom_peer(k), ray), device_id_type=MESH)
    for k in range(1, quarters):
        pl.semaphore_signal(barrier, inc=1, device_id=(me, ray_next(k)), device_id_type=MESH)

    pairs = [
        (proj_any.at[0], proj_ref),
        (taps_any, taps_ref),
        (entry_any, entry_ref),
        (place_any, place_ref),
        (slot_any, slot_ref),
        (count_any, count_ref),
        (carried_any, carried_own),
        (library_any.at[0, 0], library_ref),
        (image_any, image_ref),
    ]
    loads = [
        pltpu.make_async_copy(src, dst, load_sem.at[i]) for i, (src, dst) in enumerate(pairs)
    ]
    for copy in loads:
        copy.start()

    def dom_copy(src, dst, send, recv, k):
        return pltpu.make_async_remote_copy(
            src_ref=src,
            dst_ref=dst,
            send_sem=send.at[k],
            recv_sem=recv.at[k],
            device_id=(dom_peer(k), ray),
            device_id_type=MESH,
        )

    def ray_copy(src, dst, send, recv, slot, peer):
        return pltpu.make_async_remote_copy(
            src_ref=src,
            dst_ref=dst,
            send_sem=send.at[slot],
            recv_sem=recv.at[slot],
            device_id=(me, peer),
            device_id_type=MESH,
        )

    def block(b):
        return proj_ref[:, b * tile : (b + 1) * tile]

    loads[1].wait()
    taps_wide[...] = jnp.zeros(taps_wide.shape, f32)
    taps_wide[:, : taps_ref.shape[0]] = taps_ref[...].astype(f32)[None]
    spread = jnp.broadcast_to(taps_wide[...], (tile, taps_wide.shape[1]))
    weights = pltpu.roll(spread, half, 1, stride=1, stride_axis=0).astype(bf16)
    loads[0].wait()
    two = jnp.concatenate(
        [proj_ref[:, (b - 1) * tile : (b + 1) * tile] for b in range(1, count - 1)], axis=0
    )
    third = jnp.concatenate([block(b + 1) for b in range(1, count - 1)], axis=0)
    phase = dot(two, weights[:, : 2 * tile], NT) + dot(third, weights[:, 2 * tile :], NT)
    phase = phase.reshape(inner, owners, per, tile)
    for owner in range(owners):
        phase_out[owner, :inner] = phase[:, owner].astype(bf16)

    loads[6].wait()
    pl.semaphore_wait(barrier, owners + quarters - 2)

    halos = [
        ray_copy(
            proj_ref.at[:, pl.ds(columns - tile, tile)],
            rim.at[0],
            halo_send,
            halo_recv,
            0,
            ray_next(1),
        ),
        ray_copy(
            proj_ref.at[:, pl.ds(0, tile)], rim.at[1], halo_send, halo_recv, 1, ray_next(quarters - 1)
        ),
    ]
    for copy in halos:
        copy.start()
    phases = [
        dom_copy(
            phase_out.at[dom_peer(k), pl.ds(0, inner)],
            phase_in.at[me, pl.ds(0, inner)],
            phase_send,
            phase_recv,
            k,
        )
        for k in dom_order
    ]
    for copy in phases:
        copy.start()
    carries = [
        dom_copy(carried_own, carried_all.at[me], carried_send, carried_recv, k) for k in dom_order
    ]
    for copy in carries:
        copy.start()

    for i in range(2, 6):
        loads[i].wait()
    capacity = entry_ref.shape[1]
    alive = lax.broadcasted_iota(jnp.int32, (1, capacity), 1) < count_ref[0, 0]
    code = jnp.where(alive, slot_ref[...] * places + place_ref[...], -1)
    pick = jnp.where(
        lax.broadcasted_iota(jnp.int32, (owners * places, capacity), 0) == code, 1.0, 0.0
    ).astype(bf16)
    which = jnp.where(
        lax.broadcasted_iota(jnp.int32, (entries * SUB, capacity), 0) // SUB == entry_ref[...],
        1.0,
        0.0,
    ).astype(bf16)
    counted[...] = dot(pick, which, NT)
    diagonal = lax.rem(
        lax.broadcasted_iota(jnp.int32, (SUB, entries * SUB), 1), SUB
    ) == lax.broadcasted_iota(jnp.int32, (SUB, entries * SUB), 0)

    def widen(step, carry):
        for i in range(8):
            at = step * 8 + i
            row = jnp.broadcast_to(counted[pl.ds(at, 1), :], (SUB, entries * SUB))
            start = pl.multiple_of(at * SUB, SUB)
            spread_ref[pl.ds(start, SUB), :] = jnp.where(diagonal, row, 0.0).astype(bf16)
        return carry

    lax.fori_loop(0, owners * places // 8, widen, 0)

    loads[7].wait()

    def build(step, carry):
        first = pl.multiple_of(step * 2 * SUB, 2 * SUB)
        right = jnp.concatenate(
            [
                library_ref[:, pl.ds(first + i * SUB, SUB), :].reshape(entries * SUB, tile)
                for i in range(2)
            ],
            axis=1,
        )
        for owner in range(owners):
            rows = places * SUB
            made = dot(spread_ref[owner * rows : (owner + 1) * rows, :], right, NN)
            for place in range(places):
                for i in range(2):
                    start = pl.multiple_of(first + owner * tile + i * SUB, SUB)
                    matrix[pl.ds(start, SUB), place * tile : (place + 1) * tile] = made[
                        place * SUB : (place + 1) * SUB, i * tile : (i + 1) * tile
                    ].astype(bf16)
        return carry

    lax.fori_loop(0, tile // (2 * SUB), build, 0)

    for copy in halos:
        copy.wait()

    @pl.when(ray == 0)
    def _():
        rim[0] = jnp.zeros((slices, tile), bf16)

    @pl.when(ray == quarters - 1)
    def _():
        rim[1] = jnp.zeros((slices, tile), bf16)

    before, after = rim[0], rim[1]
    two = jnp.concatenate(
        [
            proj_ref[:, (count - 2) * tile : count * tile],
            jnp.concatenate([block(count - 1), after], axis=1),
            jnp.concatenate([before, block(0)], axis=1),
            jnp.concatenate([before, before], axis=1),
        ],
        axis=0,
    )
    third = jnp.concatenate([after, after, block(1), block(0)], axis=0)
    edge = dot(two, weights[:, : 2 * tile], NT) + dot(third, weights[:, 2 * tile :], NT)
    edge = edge.reshape(4, owners, per, tile)
    lane = lax.broadcasted_iota(jnp.int32, (owners, per, tile), 2)
    phase_out[:, inner] = edge[0].astype(bf16)
    phase_out[:, inner + 1] = jnp.where(lane < half, edge[1], edge[3]).astype(bf16)
    phase_out[:, inner + 2] = edge[2].astype(bf16)
    edges = [
        dom_copy(
            phase_out.at[dom_peer(k), pl.ds(inner, 3)],
            phase_in.at[me, pl.ds(inner, 3)],
            edge_send,
            edge_recv,
            k,
        )
        for k in dom_order
    ]
    for copy in edges:
        copy.start()
    phase_in[me] = phase_out[me]

    loads[8].wait()
    for owner in range(0, owners, 2):
        made = dot(image_ref[...], matrix[owner * tile : (owner + 2) * tile, :], NT)
        for i in range(2):
            partial_out[:, owner + i] = (
                made[:, i * tile : (i + 1) * tile].reshape(owners, per, tile).astype(bf16)
            )
    partials = [
        dom_copy(
            partial_out.at[dom_peer(k)], partial_in.at[me], partial_send, partial_recv, k
        )
        for k in dom_order
    ]
    for copy in partials:
        copy.start()
    partial_in[me] = partial_out[me]

    carried_all[me] = carried_own[...]
    for copy in carries:
        copy.wait_recv()
    to_scalar = pltpu.make_async_copy(carried_all, carried_ref, load_sem.at[len(loads)])
    to_scalar.start()
    to_scalar.wait()
    duos = [(a, b) for a in range(owners) for b in range(a + 1, owners)]

    def compare(owner, carry):
        for i, (a, b) in enumerate(duos):
            same = jnp.where(carried_ref[owner, 0, a] == carried_ref[owner, 0, b], 1.0, 0.0)
            same_ref[owner, i : i + 1, :] = jnp.full((1, tile), same, f32)
        return carry

    lax.fori_loop(0, owners, compare, 0)

    def profile_of(i):
        return median_of_eight([phase_in[a, i].astype(f32) for a in range(owners)])

    for copy in phases:
        copy.wait_recv()
    for i in range(inner):
        profile_ref[:, i * tile : (i + 1) * tile] = profile_of(i)
    for copy in edges:
        copy.wait_recv()
    for i in range(inner, ring):
        profile_ref[:, i * tile : (i + 1) * tile] = profile_of(i)

    width = ring * tile
    detector = quarters * columns
    at = lax.broadcasted_iota(jnp.int32, (1, width), 1)
    position = ray * columns + jnp.where(at < count * tile - half, at + tile, at - columns)
    profile = jnp.where((position >= 0) & (position < detector), profile_ref[...], 0.0)
    run = profile
    reach = 1
    while reach < 2 * SMOOTH:
        run = run + pltpu.roll(run, reach, 1)
        reach *= 2
    window = pltpu.roll(run, width - (SMOOTH - 1), 1) + pltpu.roll(profile, width - SMOOTH, 1)
    in_range = (
        jnp.minimum(position + SMOOTH, detector - 1) - jnp.maximum(position - SMOOTH, 0) + 1
    ).astype(f32)
    stripe = (profile - window / in_range).astype(bf16).astype(f32)
    for a in range(owners):
        for i in range(ring):
            if i != count - 1:
                fixed[a, i] = (
                    (phase_in[a, i].astype(f32) - stripe[:, i * tile : (i + 1) * tile])
                    .astype(bf16)
                    .astype(f32)
                )

    for copy in partials:
        copy.wait_recv()

    def ring_spot(b):
        return jnp.where(b == 0, ring - 1, b - 1)

    def carry_back(owner, carry):
        part = [partial_in[d, owner].astype(f32) for d in range(owners)]
        total = list(part)
        for i, (a, b) in enumerate(duos):
            same = jnp.broadcast_to(same_ref[owner, i : i + 1, :], (per, tile))
            total[a] = total[a] + same * part[b]
            total[b] = total[b] + same * part[a]
        for d in range(owners):
            back_out[d, owner] = (
                fixed[owner, ring_spot(carried_ref[owner, 0, d])] - total[d]
            ).astype(bf16)
        return carry

    lax.fori_loop(0, owners, carry_back, 0)
    backs = [
        dom_copy(back_out.at[dom_peer(k)], back_in.at[me], back_send, back_recv, k)
        for k in dom_order
    ]
    for copy in backs:
        copy.start()
    back_in[me] = back_out[me]

    def whole(owner, carry):
        part = [partial_in[d, owner].astype(f32) for d in range(owners)]
        where_to = [carried_ref[owner, 0, d] for d in range(owners)]
        for b in range(count):
            total = fixed[owner, (b - 1) % ring]
            taken = jnp.zeros((per, tile), f32)
            for d in range(owners):
                taken = taken + jnp.where(where_to[d] == b, 1.0, 0.0).astype(f32) * part[d]
            rest_out[owner, b] = (total - taken).astype(bf16)
        return carry

    lax.fori_loop(0, owners, whole, 0)
    rests = [
        dom_copy(rest_out.at[dom_peer(k)], rest_in.at[me], rest_send, rest_recv, k)
        for k in dom_order
    ]
    for copy in rests:
        copy.start()
    rest_in[me] = rest_out[me]

    updates = []
    for turn in range(2):
        held = group if turn == 0 else 1 - group
        for copy in backs[:side] if turn else backs[side:]:
            copy.wait_recv()
        first = held * side
        left = jnp.concatenate(
            [
                back_in[pl.ds(first, side), owner]
                .astype(f32)
                .reshape(rows_half, tile)
                .astype(bf16)
                for owner in range(owners)
            ],
            axis=1,
        )
        for k in (2, 3, 1, 0):
            start = pl.multiple_of(ray_twin(k) * share, share)
            made = dot(left, matrix[:, pl.ds(start, share)], NN)
            if k == 0:
                own_update[turn] = made
            else:
                update_out[turn, k] = made.astype(bf16)
                copy = ray_copy(
                    update_out.at[turn, k],
                    update_in.at[turn, k],
                    update_send,
                    update_recv,
                    turn * quarters + k,
                    ray_twin(k),
                )
                copy.start()
                updates.append(copy)

    for copy in rests:
        copy.wait_recv()
    for b in range(count):
        residual_ref[:, b * tile : (b + 1) * tile] = (
            rest_in[:, b].astype(f32).reshape(slices, tile).astype(bf16)
        )

    for turn in range(2):
        held = group if turn == 0 else 1 - group
        for copy in updates[turn * (quarters - 1) : (turn + 1) * (quarters - 1)]:
            copy.wait_recv()
        amount = own_update[turn]
        for k in range(1, quarters):
            amount = amount + update_in[turn, k].astype(f32)
        rows = pl.ds(pl.multiple_of(held * rows_half, rows_half), rows_half)
        old = image_ref[rows, pl.ds(pl.multiple_of(ray * share, share), share)].astype(f32)
        next_ref[rows, :] = old + relax_factor * amount
    for copy in carries + phases + edges + partials + backs + rests + updates:
        copy.wait_send()


def fast_shards(
    projections,
    phase_kernel,
    image,
    tile_library,
    tile_entry,
    tile_image,
    tile_slot,
    tile_count,
    slot_block,
):
    f32, bf16 = jnp.float32, jnp.bfloat16
    i32 = jnp.int32
    owners, quarters = lax.axis_size("dom"), lax.axis_size("ray")
    entries, tile = tile_library.shape[2], tile_library.shape[-1]
    _, slices, columns = projections.shape
    count = columns // tile
    ring = count + 1
    places = image.shape[0] // tile
    per = slices // owners
    capacity = tile_entry.shape[2]
    share = places * tile // quarters
    rows_half = slices // 2
    hbm = pl.BlockSpec(memory_space=pltpu.HBM)
    vmem = pl.BlockSpec(memory_space=pltpu.VMEM)
    sems = pltpu.SemaphoreType.DMA
    residual, image_next = pl.pallas_call(
        functools.partial(step_kernel, owners, quarters),
        out_shape=(
            jax.ShapeDtypeStruct((slices, columns), bf16),
            jax.ShapeDtypeStruct((slices, share), f32),
        ),
        in_specs=[hbm] * 9,
        out_specs=(vmem, vmem),
        scratch_shapes=[
            pltpu.VMEM(phase_kernel.shape, bf16),
            pltpu.VMEM((slices, columns), bf16),
            pltpu.VMEM((slices, places * tile), bf16),
            pltpu.VMEM((entries, tile, tile), bf16),
            pltpu.VMEM((1, capacity), i32),
            pltpu.VMEM((1, capacity), i32),
            pltpu.VMEM((1, capacity), i32),
            pltpu.SMEM((1, 1), i32),
            pltpu.VMEM((1, owners), i32),
            pltpu.VMEM((owners, 1, owners), i32),
            pltpu.SMEM((owners, 1, owners), i32),
            pltpu.VMEM((1, 3 * tile), f32),
            pltpu.VMEM((2, slices, tile), bf16),
            pltpu.VMEM((owners, ring, per, tile), bf16),
            pltpu.VMEM((owners, ring, per, tile), bf16),
            pltpu.VMEM((per, ring * tile), f32),
            pltpu.VMEM((owners, ring, per, tile), f32),
            pltpu.VMEM((owners * places, entries * SUB), f32),
            pltpu.VMEM((owners * places * SUB, entries * SUB), bf16),
            pltpu.VMEM((owners * tile, places * tile), bf16),
            pltpu.VMEM((owners, owners, per, tile), bf16),
            pltpu.VMEM((owners, owners, per, tile), bf16),
            pltpu.VMEM((owners, 32, tile), f32),
            pltpu.VMEM((owners, owners, per, tile), bf16),
            pltpu.VMEM((owners, owners, per, tile), bf16),
            pltpu.VMEM((owners, count, per, tile), bf16),
            pltpu.VMEM((owners, count, per, tile), bf16),
            pltpu.VMEM((2, rows_half, share), f32),
            pltpu.VMEM((2, quarters, rows_half, share), bf16),
            pltpu.VMEM((2, quarters, rows_half, share), bf16),
            sems((10,)),
            sems((2,)),
            sems((2,)),
        ]
        + [sems((owners,))] * 12
        + [sems((2 * quarters,))] * 2,
        compiler_params=pltpu.CompilerParams(
            collective_id=0, has_side_effects=True, vmem_limit_bytes=63 * 1024 * 1024
        ),
    )(
        phase_kernel,
        projections,
        image.T,
        tile_library,
        tile_entry[0],
        tile_image[0],
        tile_slot[0],
        tile_count,
        slot_block[0],
    )
    return residual[None], image_next.T


def fits_kernel(projections, phase_kernel, image, tile_library, tile_entry, *rest):
    owners, quarters = lax.axis_size("dom"), lax.axis_size("ray")
    tile = tile_library.shape[-1]
    angles, slices, columns = projections.shape
    return (
        angles == 1
        and slices % 16 == 0
        and slices == 8 * owners
        and owners == 8
        and tile == 128
        and phase_kernel.shape[0] == tile + 1
        and columns % tile == 0
        and tile_library.shape[2] == 16
        and quarters == 4
        and image.shape[0] == 16 * tile
        and tile_entry.shape[2] <= 256
    )


def any_shards(*args):
    if fits_kernel(*args):
        return fast_shards(*args)
    return shards(*args)


def solution(mesh):
    return jax.shard_map(
        any_shards,
        mesh=mesh,
        in_specs=(
            P("dom", None, "ray"),
            P(),
            P("dom", None),
            P("dom", "ray", None, None, None),
            P("dom", "ray", None),
            P("dom", "ray", None),
            P("dom", "ray", None),
            P("dom", "ray"),
            P("dom", "ray", None),
        ),
        out_specs=(P("dom", None, "ray"), P(("dom", "ray"), None)),
        check_vma=False,
    )
```

time: 44.2 us -> 33.7 us (0.76)
  Pallas kernels: 39.2 us -> 29.9 us
  local copies, waits for them, and re-layouts: 3.42 us -> 2.36 us
    pallas_call x1, Pallas kernels: 39.2 us -> 29.9 us  [fast_shards(): pl.pallas_call(functools.partial(step_kernel, owners, quarters), out_shap...]
    broadcast_in_dim x1 -> x0, local copies, waits for them, and re-layouts: 0.66 us -> none  [fast_shards(): phase_kernel[None]]
    unnamed x15 -> x4, local copies, waits for them, and re-layouts: 2.76 us -> 2.36 us
where the time goes in v1:
time: 33.7 us; the launch traced here: 33.6 us
  Pallas kernels  29.9 us (89%)
  local copies, waits for them, and re-layouts  2.36 us (7%)
  between operations  1.3 us (4%)
    pallas_call x1, Pallas kernels, fast_shards(): pl.pallas_call(functools.partial(step_kernel, owners, quarters), out_shap...  29.9 us
    unnamed x4, local copies, waits for them, and re-layouts  2.36 us

profile of v1, /device:TPU:0, one launch (start us, length us, event | category | flops | bytes accessed | tf_op | source)
XLA Modules:
  0.0 33.6 jit_solution(8332190683305846442)
XLA Ops:
  1.3 29.9 %shard_map.104 = (bf16[64,2048]{1,0:T(8,128)(2,1)}, f32[64,512]{1,0:T(8,128)}) custom-call(bf16[129]{0:T(256)(128)(2,1)} %taps_any.1, bf16[1,64,2048]{2,1,0:T(8,128)(2,1)} %proj_any.1, bf16[64,2048]{1,0:T(8,128)(2,1)} %bitcast.8, bf16[1,1,16,128,128]{4,3,2,1,0:T(8,128)(2,1)} %library_any.1, s32[1,256]{1,0:T(1,128)} %bitcast.10, s32[1,256]{1,0:T(1,128)} %bitcast.11, ...), custom_call_target="tpu_custom_call" | custom-call | tf_op jit(solution)/shard_map/pallas_call | solution.py:681
  31.2 0.0 copy-start
  31.2 1.7 %copy.14 = bf16[1,64,2048]{2,1,0:T(8,128)(2,1)} copy(bf16[1,64,2048]{2,1,0:T(8,128)(2,1)} %bitcast.7) | data formatting | bytes 524288
  32.9 0.0 copy-done
  32.9 0.7 %copy.15 = f32[512,64]{0,1:T(8,128)} copy(f32[512,64]{0,1:T(8,128)S(1)} %bitcast.9) | data formatting | bytes 262144
Async XLA Ops:
  31.2 1.7 %copy-start = (f32[64,512]{1,0:T(8,128)S(1)}, f32[64,512]{1,0:T(8,128)}, u32[]{:S(2)}) copy-start(f32[64,512]{1,0:T(8,128)} %get-tuple-element.5) | copy-start | bytes 393220

commit v2 on v1

--- a/solution.py
+++ b/solution.py
@@ -204,8 +204,8 @@
     entry_any,
     place_any,
     slot_any,
-    count_any,
     carried_any,
+    count_ref,
     residual_ref,
     next_ref,
     taps_ref,
@@ -215,7 +215,6 @@
     entry_ref,
     place_ref,
     slot_ref,
-    count_ref,
     carried_own,
     carried_all,
     carried_ref,
@@ -277,7 +276,7 @@
             return (1 - group) * side + lax.rem(spot + k - side, side)
         return group * side + lax.rem(spot + k, side)
 
-    dom_order = list(range(side, owners)) + list(range(1, side))
+    dom_order = list(range(1, owners))
 
     chip, core = ray // 2, lax.rem(ray, 2)
 
@@ -301,7 +300,6 @@
         (entry_any, entry_ref),
         (place_any, place_ref),
         (slot_any, slot_ref),
-        (count_any, count_ref),
         (carried_any, carried_own),
         (library_any.at[0, 0], library_ref),
         (image_any, image_ref),
@@ -350,8 +348,14 @@
     for owner in range(owners):
         phase_out[owner, :inner] = phase[:, owner].astype(bf16)
 
-    loads[6].wait()
+    loads[5].wait()
     pl.semaphore_wait(barrier, owners + quarters - 2)
+
+    carries = [
+        dom_copy(carried_own, carried_all.at[me], carried_send, carried_recv, k) for k in dom_order
+    ]
+    for copy in carries:
+        copy.start()
 
     halos = [
         ray_copy(
@@ -380,13 +384,7 @@
     ]
     for copy in phases:
         copy.start()
-    carries = [
-        dom_copy(carried_own, carried_all.at[me], carried_send, carried_recv, k) for k in dom_order
-    ]
-    for copy in carries:
-        copy.start()
-
-    for i in range(2, 6):
+    for i in range(2, 5):
         loads[i].wait()
     capacity = entry_ref.shape[1]
     alive = lax.broadcasted_iota(jnp.int32, (1, capacity), 1) < count_ref[0, 0]
@@ -414,7 +412,7 @@
 
     lax.fori_loop(0, owners * places // 8, widen, 0)
 
-    loads[7].wait()
+    loads[6].wait()
 
     def build(step, carry):
         first = pl.multiple_of(step * 2 * SUB, 2 * SUB)
@@ -480,7 +478,7 @@
         copy.start()
     phase_in[me] = phase_out[me]
 
-    loads[8].wait()
+    loads[7].wait()
     for owner in range(0, owners, 2):
         made = dot(image_ref[...], matrix[owner * tile : (owner + 2) * tile, :], NT)
         for i in range(2):
@@ -600,7 +598,7 @@
     updates = []
     for turn in range(2):
         held = group if turn == 0 else 1 - group
-        for copy in backs[:side] if turn else backs[side:]:
+        for copy in backs[side - 1 :] if turn else backs[: side - 1]:
             copy.wait_recv()
         first = held * side
         left = jnp.concatenate(
@@ -684,7 +682,7 @@
             jax.ShapeDtypeStruct((slices, columns), bf16),
             jax.ShapeDtypeStruct((slices, share), f32),
         ),
-        in_specs=[hbm] * 9,
+        in_specs=[hbm] * 8 + [pl.BlockSpec(memory_space=pltpu.SMEM)],
         out_specs=(vmem, vmem),
         scratch_shapes=[
             pltpu.VMEM(phase_kernel.shape, bf16),
@@ -694,7 +692,6 @@
             pltpu.VMEM((1, capacity), i32),
             pltpu.VMEM((1, capacity), i32),
             pltpu.VMEM((1, capacity), i32),
-            pltpu.SMEM((1, 1), i32),
             pltpu.VMEM((1, owners), i32),
             pltpu.VMEM((owners, 1, owners), i32),
             pltpu.SMEM((owners, 1, owners), i32),
@@ -724,18 +721,23 @@
         + [sems((owners,))] * 12
         + [sems((2 * quarters,))] * 2,
         compiler_params=pltpu.CompilerParams(
-            collective_id=0, has_side_effects=True, vmem_limit_bytes=63 * 1024 * 1024
+            collective_id=0, has_side_effects=True, vmem_limit_bytes=48 * 1024 * 1024
         ),
     )(
-        phase_kernel,
-        projections,
-        image.T,
-        tile_library,
-        tile_entry[0],
-        tile_image[0],
-        tile_slot[0],
+        *[
+            pltpu.with_memory_space_constraint(x, pltpu.HBM)
+            for x in (
+                phase_kernel,
+                projections,
+                image.T,
+                tile_library,
+                tile_entry[0],
+                tile_image[0],
+                tile_slot[0],
+                slot_block[0],
+            )
+        ],
         tile_count,
-        slot_block[0],
     )
     return residual[None], image_next.T
 

time: 33.7 us -> 31.6 us (0.938)
  Pallas kernels: 29.9 us -> 28.8 us
  local copies, waits for them, and re-layouts: 2.36 us -> 1.36 us
    pallas_call x1, Pallas kernels: 29.9 us -> 28.8 us  [fast_shards(): pl.pallas_call(functools.partial(step_kernel, owners, quarters), out_shap...]
    unnamed x4 -> x2, local copies, waits for them, and re-layouts: 2.36 us -> 1.36 us
where the time goes in v2:
time: 31.6 us; the launch traced here: 31.4 us
  Pallas kernels  28.8 us (91%)
  local copies, waits for them, and re-layouts  1.36 us (4%)
  between operations  1.29 us (4%)
    pallas_call x1, Pallas kernels, fast_shards(): pl.pallas_call(functools.partial(step_kernel, owners, quarters), out_shap...  28.8 us
    unnamed x2, local copies, waits for them, and re-layouts  1.36 us

profile of v2, /device:TPU:0, one launch (start us, length us, event | category | flops | bytes accessed | tf_op | source)
XLA Modules:
  0.0 31.4 jit_solution(11862041224018668491)
XLA Ops:
  1.3 28.8 %shard_map.104 = (bf16[64,2048]{1,0:T(8,128)(2,1)S(1)}, f32[64,512]{1,0:T(8,128)S(1)}) custom-call(bf16[129]{0:T(256)(128)(2,1)} %taps_any.1, bf16[1,64,2048]{2,1,0:T(8,128)(2,1)} %proj_any.1, bf16[64,2048]{1,0:T(8,128)(2,1)} %bitcast.9, bf16[1,1,16,128,128]{4,3,2,1,0:T(8,128)(2,1)} %library_any.1, s32[1,256]{1,0:T(1,128)} %bitcast.10, s32[1,256]{1,0:T(1,128)} %bitcast.11, ...), custom_call_target="tpu_custom_call" | custom-call | tf_op jit(solution)/shard_map/pallas_call | solution.py:679
  30.1 0.7 %copy.14 = bf16[1,64,2048]{2,1,0:T(8,128)(2,1)} copy(bf16[1,64,2048]{2,1,0:T(8,128)(2,1)S(1)} %bitcast.7) | data formatting | bytes 524288
  30.8 0.7 %copy.15 = f32[512,64]{0,1:T(8,128)} copy(f32[512,64]{0,1:T(8,128)S(1)} %bitcast.8) | data formatting | bytes 262144

commit v3 on v2

--- a/solution.py
+++ b/solution.py
@@ -165,6 +165,7 @@
 NT = (((1,), (1,)), ((), ()))
 NN = (((1,), (0,)), ((), ()))
 SUB = 16
+PARTS = 2
 
 
 def dot(a, b, dims):
@@ -234,6 +235,11 @@
     back_in,
     rest_out,
     rest_in,
+    stripe_own,
+    stripe_far,
+    twin_in,
+    forward,
+    gathered,
     own_update,
     update_out,
     update_in,
@@ -252,6 +258,10 @@
     back_recv,
     rest_send,
     rest_recv,
+    stripe_send,
+    stripe_recv,
+    twin_send,
+    twin_recv,
     update_send,
     update_recv,
 ):
@@ -268,6 +278,7 @@
     half = tile // 2
     share = places * tile // quarters
     rows_half = side * per
+    some = owners // PARTS
 
     group, spot = me // side, lax.rem(me, side)
 
@@ -310,12 +321,12 @@
     for copy in loads:
         copy.start()
 
-    def dom_copy(src, dst, send, recv, k):
+    def dom_copy(src, dst, send, recv, k, base=0):
         return pltpu.make_async_remote_copy(
             src_ref=src,
             dst_ref=dst,
-            send_sem=send.at[k],
-            recv_sem=recv.at[k],
+            send_sem=send.at[base + k],
+            recv_sem=recv.at[base + k],
             device_id=(dom_peer(k), ray),
             device_id_type=MESH,
         )
@@ -479,20 +490,30 @@
     phase_in[me] = phase_out[me]
 
     loads[7].wait()
-    for owner in range(0, owners, 2):
-        made = dot(image_ref[...], matrix[owner * tile : (owner + 2) * tile, :], NT)
-        for i in range(2):
-            partial_out[:, owner + i] = (
-                made[:, i * tile : (i + 1) * tile].reshape(owners, per, tile).astype(bf16)
-            )
-    partials = [
-        dom_copy(
-            partial_out.at[dom_peer(k)], partial_in.at[me], partial_send, partial_recv, k
-        )
-        for k in dom_order
-    ]
-    for copy in partials:
-        copy.start()
+    partials = []
+    for part in range(PARTS):
+        for owner in range(part * some, (part + 1) * some, 2):
+            made = dot(image_ref[...], matrix[owner * tile : (owner + 2) * tile, :], NT)
+            for i in range(2):
+                partial_out[:, owner + i] = (
+                    made[:, i * tile : (i + 1) * tile].reshape(owners, per, tile).astype(bf16)
+                )
+        chosen = pl.ds(part * some, some)
+        partials.append(
+            [
+                dom_copy(
+                    partial_out.at[dom_peer(k), chosen],
+                    partial_in.at[me, chosen],
+                    partial_send,
+                    partial_recv,
+                    k,
+                    part * owners,
+                )
+                for k in dom_order
+            ]
+        )
+        for copy in partials[part]:
+            copy.start()
     partial_in[me] = partial_out[me]
 
     carried_all[me] = carried_own[...]
@@ -538,6 +559,9 @@
         jnp.minimum(position + SMOOTH, detector - 1) - jnp.maximum(position - SMOOTH, 0) + 1
     ).astype(f32)
     stripe = (profile - window / in_range).astype(bf16).astype(f32)
+    for b in range(count):
+        i = (b - 1) % ring
+        stripe_own[b] = stripe[:, i * tile : (i + 1) * tile].astype(bf16)
     for a in range(owners):
         for i in range(ring):
             if i != count - 1:
@@ -546,9 +570,6 @@
                     .astype(bf16)
                     .astype(f32)
                 )
-
-    for copy in partials:
-        copy.wait_recv()
 
     def ring_spot(b):
         return jnp.where(b == 0, ring - 1, b - 1)
@@ -566,16 +587,47 @@
             ).astype(bf16)
         return carry
 
-    lax.fori_loop(0, owners, carry_back, 0)
-    backs = [
-        dom_copy(back_out.at[dom_peer(k)], back_in.at[me], back_send, back_recv, k)
+    backs = []
+    for part in range(PARTS):
+        for copy in partials[part]:
+            copy.wait_recv()
+        lax.fori_loop(part * some, (part + 1) * some, carry_back, 0)
+        chosen = pl.ds(part * some, some)
+        backs.append(
+            [
+                dom_copy(
+                    back_out.at[dom_peer(k), chosen],
+                    back_in.at[me, chosen],
+                    back_send,
+                    back_recv,
+                    k,
+                    part * owners,
+                )
+                for k in dom_order
+            ]
+        )
+        for copy in backs[part]:
+            copy.start()
+    back_in[me] = back_out[me]
+
+    crossing = dom_copy(stripe_own, stripe_far.at[spot], stripe_send, stripe_recv, side)
+    crossing.start()
+    twins = [
+        dom_copy(
+            partial_out.at[pl.ds((1 - dom_peer(k) // side) * side, side), dom_peer(k)],
+            twin_in.at[me],
+            twin_send,
+            twin_recv,
+            k,
+        )
         for k in dom_order
     ]
-    for copy in backs:
+    for copy in twins:
         copy.start()
-    back_in[me] = back_out[me]
-
-    def whole(owner, carry):
+    twin_in[me] = partial_out[pl.ds((1 - group) * side, side), me]
+
+    def whole(i, carry):
+        owner = group * side + i
         part = [partial_in[d, owner].astype(f32) for d in range(owners)]
         where_to = [carried_ref[owner, 0, d] for d in range(owners)]
         for b in range(count):
@@ -583,52 +635,87 @@
             taken = jnp.zeros((per, tile), f32)
             for d in range(owners):
                 taken = taken + jnp.where(where_to[d] == b, 1.0, 0.0).astype(f32) * part[d]
-            rest_out[owner, b] = (total - taken).astype(bf16)
+            rest_out[i, b] = (total - taken).astype(bf16)
         return carry
 
-    lax.fori_loop(0, owners, whole, 0)
+    lax.fori_loop(0, side, whole, 0)
     rests = [
-        dom_copy(rest_out.at[dom_peer(k)], rest_in.at[me], rest_send, rest_recv, k)
-        for k in dom_order
+        dom_copy(
+            rest_out.at[lax.rem(spot + k, side)], rest_in.at[me], rest_send, rest_recv, k
+        )
+        for k in range(1, side)
     ]
     for copy in rests:
         copy.start()
-    rest_in[me] = rest_out[me]
+    rest_in[me] = rest_out[spot]
 
     updates = []
     for turn in range(2):
         held = group if turn == 0 else 1 - group
-        for copy in backs[side - 1 :] if turn else backs[: side - 1]:
-            copy.wait_recv()
         first = held * side
-        left = jnp.concatenate(
-            [
-                back_in[pl.ds(first, side), owner]
-                .astype(f32)
-                .reshape(rows_half, tile)
-                .astype(bf16)
-                for owner in range(owners)
-            ],
-            axis=1,
-        )
-        for k in (2, 3, 1, 0):
-            start = pl.multiple_of(ray_twin(k) * share, share)
-            made = dot(left, matrix[:, pl.ds(start, share)], NN)
-            if k == 0:
-                own_update[turn] = made
-            else:
-                update_out[turn, k] = made.astype(bf16)
-                copy = ray_copy(
-                    update_out.at[turn, k],
-                    update_in.at[turn, k],
-                    update_send,
-                    update_recv,
-                    turn * quarters + k,
-                    ray_twin(k),
-                )
-                copy.start()
-                updates.append(copy)
-
+        for part in range(PARTS):
+            for copy in backs[part][side - 1 :] if turn else backs[part][: side - 1]:
+                copy.wait_recv()
+            left = jnp.concatenate(
+                [
+                    back_in[pl.ds(first, side), owner]
+                    .astype(f32)
+                    .reshape(rows_half, tile)
+                    .astype(bf16)
+                    for owner in range(part * some, (part + 1) * some)
+                ],
+                axis=1,
+            )
+            rows = slice(part * some * tile, (part + 1) * some * tile)
+            for k in (2, 3, 1, 0):
+                start = pl.multiple_of(ray_twin(k) * share, share)
+                made = dot(left, matrix[rows, pl.ds(start, share)], NN)
+                if part > 0:
+                    made = made + gathered[k]
+                if part < PARTS - 1:
+                    gathered[k] = made
+                elif k == 0:
+                    own_update[turn] = made
+                else:
+                    update_out[turn, k] = made.astype(bf16)
+                    copy = ray_copy(
+                        update_out.at[turn, k],
+                        update_in.at[turn, k],
+                        update_send,
+                        update_recv,
+                        turn * quarters + k,
+                        ray_twin(k),
+                    )
+                    copy.start()
+                    updates.append(copy)
+
+    crossing.wait_recv()
+    relays = [
+        dom_copy(stripe_far.at[spot], stripe_far.at[spot], stripe_send, stripe_recv, k)
+        for k in range(1, side)
+    ]
+    for copy in relays:
+        copy.start()
+
+    for copy in twins:
+        copy.wait_recv()
+    other = pl.ds((1 - group) * side, side)
+    own_spots = [carried_ref[me, 0, d] for d in range(owners)]
+    taken_by = [twin_in[d].astype(f32) for d in range(owners)]
+    for b in range(count):
+        taken = jnp.zeros((side, per, tile), f32)
+        for d in range(owners):
+            taken = taken + jnp.where(own_spots[d] == b, 1.0, 0.0).astype(f32) * taken_by[d]
+        forward[b] = taken
+    for copy in relays:
+        copy.wait_recv()
+    for b in range(count):
+        clean = (
+            (phase_out[other, (b - 1) % ring].astype(f32) - stripe_far[:, b].astype(f32))
+            .astype(bf16)
+            .astype(f32)
+        )
+        rest_in[other, b] = (clean - forward[b]).astype(bf16)
     for copy in rests:
         copy.wait_recv()
     for b in range(count):
@@ -646,8 +733,20 @@
         rows = pl.ds(pl.multiple_of(held * rows_half, rows_half), rows_half)
         old = image_ref[rows, pl.ds(pl.multiple_of(ray * share, share), share)].astype(f32)
         next_ref[rows, :] = old + relax_factor * amount
-    for copy in carries + phases + edges + partials + backs + rests + updates:
+    sent = carries + phases + edges + sum(partials, []) + sum(backs, [])
+    for copy in sent + [crossing] + twins + rests + relays + updates:
         copy.wait_send()
+
+
+def store_kernel(residual_ref, next_ref, residual_out, next_out, sem):
+    copies = [
+        pltpu.make_async_copy(residual_ref, residual_out, sem.at[0]),
+        pltpu.make_async_copy(next_ref, next_out, sem.at[1]),
+    ]
+    for copy in copies:
+        copy.start()
+    for copy in copies:
+        copy.wait()
 
 
 def fast_shards(
@@ -709,8 +808,13 @@
             pltpu.VMEM((owners, 32, tile), f32),
             pltpu.VMEM((owners, owners, per, tile), bf16),
             pltpu.VMEM((owners, owners, per, tile), bf16),
+            pltpu.VMEM((owners // 2, count, per, tile), bf16),
             pltpu.VMEM((owners, count, per, tile), bf16),
-            pltpu.VMEM((owners, count, per, tile), bf16),
+            pltpu.VMEM((count, per, tile), bf16),
+            pltpu.VMEM((owners // 2, count, per, tile), bf16),
+            pltpu.VMEM((owners, owners // 2, per, tile), bf16),
+            pltpu.VMEM((count, owners // 2, per, tile), f32),
+            pltpu.VMEM((quarters, rows_half, share), f32),
             pltpu.VMEM((2, rows_half, share), f32),
             pltpu.VMEM((2, quarters, rows_half, share), bf16),
             pltpu.VMEM((2, quarters, rows_half, share), bf16),
@@ -718,7 +822,9 @@
             sems((2,)),
             sems((2,)),
         ]
-        + [sems((owners,))] * 12
+        + [sems((owners,))] * 6
+        + [sems((PARTS * owners,))] * 4
+        + [sems((owners,))] * 6
         + [sems((2 * quarters,))] * 2,
         compiler_params=pltpu.CompilerParams(
             collective_id=0, has_side_effects=True, vmem_limit_bytes=48 * 1024 * 1024
@@ -739,6 +845,19 @@
         ],
         tile_count,
     )
+    residual, image_next = pl.pallas_call(
+        store_kernel,
+        out_shape=(
+            jax.ShapeDtypeStruct(residual.shape, bf16),
+            jax.ShapeDtypeStruct(image_next.shape, f32),
+        ),
+        in_specs=[pl.BlockSpec(memory_space=pl.ANY)] * 2,
+        out_specs=[pl.BlockSpec(memory_space=pl.ANY)] * 2,
+        scratch_shapes=[sems((2,))],
+    )(
+        pltpu.with_memory_space_constraint(residual, pltpu.VMEM),
+        pltpu.with_memory_space_constraint(image_next, pltpu.VMEM),
+    )
     return residual[None], image_next.T
 
 

time: 31.6 us -> 30.4 us (0.962)
  local copies, waits for them, and re-layouts: 1.36 us -> 0 us
    unnamed x2 -> x0, local copies, waits for them, and re-layouts: 1.36 us -> none
    pallas_call x0 -> x1, Pallas kernels: none -> 0.76 us  [fast_shards(): pl.pallas_call(store_kernel, out_shape=(jax.ShapeDtypeStruct(residual.sha...]
    pallas_call x1, Pallas kernels: 28.8 us -> 28.2 us  [fast_shards(): pl.pallas_call(functools.partial(step_kernel, owners, quarters), out_shap...]
where the time goes in v3:
time: 30.4 us; the launch traced here: 30.2 us
  Pallas kernels  28.9 us (95%)
  between operations  1.29 us (4%)
    pallas_call x1, Pallas kernels, fast_shards(): pl.pallas_call(functools.partial(step_kernel, owners, quarters), out_shap...  28.2 us
    pallas_call x1, Pallas kernels, fast_shards(): pl.pallas_call(store_kernel, out_shape=(jax.ShapeDtypeStruct(residual.sha...  0.76 us

profile of v3, /device:TPU:0, one launch (start us, length us, event | category | flops | bytes accessed | tf_op | source)
XLA Modules:
  0.0 30.2 jit_solution(18436916978185634556)
XLA Ops:
  1.3 28.2 %shard_map.104 = (bf16[64,2048]{1,0:T(8,128)(2,1)S(1)}, f32[64,512]{1,0:T(8,128)S(1)}) custom-call(bf16[129]{0:T(256)(128)(2,1)} %taps_any.1, bf16[1,64,2048]{2,1,0:T(8,128)(2,1)} %proj_any.1, bf16[64,2048]{1,0:T(8,128)(2,1)} %bitcast.7, bf16[1,1,16,128,128]{4,3,2,1,0:T(8,128)(2,1)} %library_any.1, s32[1,256]{1,0:T(1,128)} %bitcast.8, s32[1,256]{1,0:T(1,128)} %bitcast.9, ...), custom_call_target="tpu_custom_call" | custom-call | tf_op jit(solution)/shard_map/pallas_call | solution.py:778
  29.4 0.8 %shard_map.105 = (bf16[64,2048]{1,0:T(8,128)(2,1)}, f32[64,512]{1,0:T(8,128)}) custom-call(bf16[64,2048]{1,0:T(8,128)(2,1)S(1)} %get-tuple-element.6.residual_ref, f32[64,512]{1,0:T(8,128)S(1)} %get-tuple-element.7.next_ref), custom_call_target="tpu_custom_call" | custom-call | tf_op jit(solution)/shard_map/pallas_call | solution.py:848

commit v4 on v3

--- a/solution.py
+++ b/solution.py
@@ -213,9 +213,7 @@
     proj_ref,
     image_ref,
     library_ref,
-    entry_ref,
-    place_ref,
-    slot_ref,
+    lists_ref,
     carried_own,
     carried_all,
     carried_ref,
@@ -250,8 +248,6 @@
     carried_recv,
     phase_send,
     phase_recv,
-    edge_send,
-    edge_recv,
     partial_send,
     partial_recv,
     back_send,
@@ -306,50 +302,50 @@
         pl.semaphore_signal(barrier, inc=1, device_id=(me, ray_next(k)), device_id_type=MESH)
 
     pairs = [
-        (proj_any.at[0], proj_ref),
-        (taps_any, taps_ref),
-        (entry_any, entry_ref),
-        (place_any, place_ref),
-        (slot_any, slot_ref),
-        (carried_any, carried_own),
-        (library_any.at[0, 0], library_ref),
-        (image_any, image_ref),
+        (proj_any.at[0], proj_ref, 0),
+        (taps_any, taps_ref, 1),
+        (carried_any, carried_own, 2),
+        (entry_any, lists_ref.at[0], 3),
+        (place_any, lists_ref.at[1], 3),
+        (slot_any, lists_ref.at[2], 3),
+        (library_any.at[0, 0], library_ref, 4),
+        (image_any, image_ref, 5),
     ]
-    loads = [
-        pltpu.make_async_copy(src, dst, load_sem.at[i]) for i, (src, dst) in enumerate(pairs)
-    ]
-    for copy in loads:
-        copy.start()
-
-    def dom_copy(src, dst, send, recv, k, base=0):
-        return pltpu.make_async_remote_copy(
+    for src, dst, i in pairs:
+        pltpu.make_async_copy(src, dst, load_sem.at[i]).start()
+
+    def await_bytes(ref, sem):
+        pltpu.make_async_copy(ref, ref, sem).wait()
+
+    def dom_copy(src, dst, send, recv, k):
+        pltpu.make_async_remote_copy(
             src_ref=src,
             dst_ref=dst,
-            send_sem=send.at[base + k],
-            recv_sem=recv.at[base + k],
+            send_sem=send,
+            recv_sem=recv,
             device_id=(dom_peer(k), ray),
             device_id_type=MESH,
-        )
-
-    def ray_copy(src, dst, send, recv, slot, peer):
-        return pltpu.make_async_remote_copy(
+        ).start()
+
+    def ray_copy(src, dst, send, recv, peer):
+        pltpu.make_async_remote_copy(
             src_ref=src,
             dst_ref=dst,
-            send_sem=send.at[slot],
-            recv_sem=recv.at[slot],
+            send_sem=send,
+            recv_sem=recv,
             device_id=(me, peer),
             device_id_type=MESH,
-        )
+        ).start()
 
     def block(b):
         return proj_ref[:, b * tile : (b + 1) * tile]
 
-    loads[1].wait()
+    await_bytes(taps_ref, load_sem.at[1])
     taps_wide[...] = jnp.zeros(taps_wide.shape, f32)
     taps_wide[:, : taps_ref.shape[0]] = taps_ref[...].astype(f32)[None]
     spread = jnp.broadcast_to(taps_wide[...], (tile, taps_wide.shape[1]))
     weights = pltpu.roll(spread, half, 1, stride=1, stride_axis=0).astype(bf16)
-    loads[0].wait()
+    await_bytes(proj_ref, load_sem.at[0])
     two = jnp.concatenate(
         [proj_ref[:, (b - 1) * tile : (b + 1) * tile] for b in range(1, count - 1)], axis=0
     )
@@ -359,52 +355,44 @@
     for owner in range(owners):
         phase_out[owner, :inner] = phase[:, owner].astype(bf16)
 
-    loads[5].wait()
+    await_bytes(carried_own, load_sem.at[2])
     pl.semaphore_wait(barrier, owners + quarters - 2)
 
-    carries = [
-        dom_copy(carried_own, carried_all.at[me], carried_send, carried_recv, k) for k in dom_order
-    ]
-    for copy in carries:
-        copy.start()
-
-    halos = [
-        ray_copy(
-            proj_ref.at[:, pl.ds(columns - tile, tile)],
-            rim.at[0],
-            halo_send,
-            halo_recv,
-            0,
-            ray_next(1),
-        ),
-        ray_copy(
-            proj_ref.at[:, pl.ds(0, tile)], rim.at[1], halo_send, halo_recv, 1, ray_next(quarters - 1)
-        ),
-    ]
-    for copy in halos:
-        copy.start()
-    phases = [
+    for k in dom_order:
+        dom_copy(carried_own, carried_all.at[me], carried_send.at[0], carried_recv.at[0], k)
+    ray_copy(
+        proj_ref.at[:, pl.ds(columns - tile, tile)],
+        rim.at[0],
+        halo_send.at[0],
+        halo_recv.at[0],
+        ray_next(1),
+    )
+    ray_copy(
+        proj_ref.at[:, pl.ds(0, tile)],
+        rim.at[1],
+        halo_send.at[0],
+        halo_recv.at[0],
+        ray_next(quarters - 1),
+    )
+    for k in dom_order:
         dom_copy(
             phase_out.at[dom_peer(k), pl.ds(0, inner)],
             phase_in.at[me, pl.ds(0, inner)],
-            phase_send,
-            phase_recv,
+            phase_send.at[0],
+            phase_recv.at[0],
             k,
         )
-        for k in dom_order
-    ]
-    for copy in phases:
-        copy.start()
-    for i in range(2, 5):
-        loads[i].wait()
-    capacity = entry_ref.shape[1]
+
+    await_bytes(lists_ref, load_sem.at[3])
+    capacity = lists_ref.shape[2]
+    entry, place, slot = lists_ref[0], lists_ref[1], lists_ref[2]
     alive = lax.broadcasted_iota(jnp.int32, (1, capacity), 1) < count_ref[0, 0]
-    code = jnp.where(alive, slot_ref[...] * places + place_ref[...], -1)
+    code = jnp.where(alive, slot * places + place, -1)
     pick = jnp.where(
         lax.broadcasted_iota(jnp.int32, (owners * places, capacity), 0) == code, 1.0, 0.0
     ).astype(bf16)
     which = jnp.where(
-        lax.broadcasted_iota(jnp.int32, (entries * SUB, capacity), 0) // SUB == entry_ref[...],
+        lax.broadcasted_iota(jnp.int32, (entries * SUB, capacity), 0) // SUB == entry,
         1.0,
         0.0,
     ).astype(bf16)
@@ -423,7 +411,7 @@
 
     lax.fori_loop(0, owners * places // 8, widen, 0)
 
-    loads[6].wait()
+    await_bytes(library_ref, load_sem.at[4])
 
     def build(step, carry):
         first = pl.multiple_of(step * 2 * SUB, 2 * SUB)
@@ -447,8 +435,7 @@
 
     lax.fori_loop(0, tile // (2 * SUB), build, 0)
 
-    for copy in halos:
-        copy.wait()
+    await_bytes(rim, halo_recv.at[0])
 
     @pl.when(ray == 0)
     def _():
@@ -475,22 +462,17 @@
     phase_out[:, inner] = edge[0].astype(bf16)
     phase_out[:, inner + 1] = jnp.where(lane < half, edge[1], edge[3]).astype(bf16)
     phase_out[:, inner + 2] = edge[2].astype(bf16)
-    edges = [
+    for k in dom_order:
         dom_copy(
             phase_out.at[dom_peer(k), pl.ds(inner, 3)],
             phase_in.at[me, pl.ds(inner, 3)],
-            edge_send,
-            edge_recv,
+            phase_send.at[1],
+            phase_recv.at[1],
             k,
         )
-        for k in dom_order
-    ]
-    for copy in edges:
-        copy.start()
     phase_in[me] = phase_out[me]
 
-    loads[7].wait()
-    partials = []
+    await_bytes(image_ref, load_sem.at[5])
     for part in range(PARTS):
         for owner in range(part * some, (part + 1) * some, 2):
             made = dot(image_ref[...], matrix[owner * tile : (owner + 2) * tile, :], NT)
@@ -499,27 +481,19 @@
                     made[:, i * tile : (i + 1) * tile].reshape(owners, per, tile).astype(bf16)
                 )
         chosen = pl.ds(part * some, some)
-        partials.append(
-            [
-                dom_copy(
-                    partial_out.at[dom_peer(k), chosen],
-                    partial_in.at[me, chosen],
-                    partial_send,
-                    partial_recv,
-                    k,
-                    part * owners,
-                )
-                for k in dom_order
-            ]
-        )
-        for copy in partials[part]:
-            copy.start()
+        for k in dom_order:
+            dom_copy(
+                partial_out.at[dom_peer(k), chosen],
+                partial_in.at[me, chosen],
+                partial_send.at[0],
+                partial_recv.at[part],
+                k,
+            )
     partial_in[me] = partial_out[me]
 
     carried_all[me] = carried_own[...]
-    for copy in carries:
-        copy.wait_recv()
-    to_scalar = pltpu.make_async_copy(carried_all, carried_ref, load_sem.at[len(loads)])
+    await_bytes(carried_all.at[pl.ds(0, owners - 1)], carried_recv.at[0])
+    to_scalar = pltpu.make_async_copy(carried_all, carried_ref, load_sem.at[6])
     to_scalar.start()
     to_scalar.wait()
     duos = [(a, b) for a in range(owners) for b in range(a + 1, owners)]
@@ -535,12 +509,11 @@
     def profile_of(i):
         return median_of_eight([phase_in[a, i].astype(f32) for a in range(owners)])
 
-    for copy in phases:
-        copy.wait_recv()
+    others = pl.ds(0, owners - 1)
+    await_bytes(phase_in.at[others, pl.ds(0, inner)], phase_recv.at[0])
     for i in range(inner):
         profile_ref[:, i * tile : (i + 1) * tile] = profile_of(i)
-    for copy in edges:
-        copy.wait_recv()
+    await_bytes(phase_in.at[others, pl.ds(inner, 3)], phase_recv.at[1])
     for i in range(inner, ring):
         profile_ref[:, i * tile : (i + 1) * tile] = profile_of(i)
 
@@ -587,43 +560,29 @@
             ).astype(bf16)
         return carry
 
-    backs = []
     for part in range(PARTS):
-        for copy in partials[part]:
-            copy.wait_recv()
+        chosen = pl.ds(part * some, some)
+        await_bytes(partial_in.at[others, chosen], partial_recv.at[part])
         lax.fori_loop(part * some, (part + 1) * some, carry_back, 0)
-        chosen = pl.ds(part * some, some)
-        backs.append(
-            [
-                dom_copy(
-                    back_out.at[dom_peer(k), chosen],
-                    back_in.at[me, chosen],
-                    back_send,
-                    back_recv,
-                    k,
-                    part * owners,
-                )
-                for k in dom_order
-            ]
-        )
-        for copy in backs[part]:
-            copy.start()
+        for k in dom_order:
+            dom_copy(
+                back_out.at[dom_peer(k), chosen],
+                back_in.at[me, chosen],
+                back_send.at[0],
+                back_recv.at[part * 2 + k // side],
+                k,
+            )
     back_in[me] = back_out[me]
 
-    crossing = dom_copy(stripe_own, stripe_far.at[spot], stripe_send, stripe_recv, side)
-    crossing.start()
-    twins = [
+    dom_copy(stripe_own, stripe_far.at[spot], stripe_send.at[0], stripe_recv.at[0], side)
+    for k in dom_order:
         dom_copy(
             partial_out.at[pl.ds((1 - dom_peer(k) // side) * side, side), dom_peer(k)],
             twin_in.at[me],
-            twin_send,
-            twin_recv,
+            twin_send.at[0],
+            twin_recv.at[0],
             k,
         )
-        for k in dom_order
-    ]
-    for copy in twins:
-        copy.start()
     twin_in[me] = partial_out[pl.ds((1 - group) * side, side), me]
 
     def whole(i, carry):
@@ -639,23 +598,24 @@
         return carry
 
     lax.fori_loop(0, side, whole, 0)
-    rests = [
+    for k in range(1, side):
         dom_copy(
-            rest_out.at[lax.rem(spot + k, side)], rest_in.at[me], rest_send, rest_recv, k
-        )
-        for k in range(1, side)
-    ]
-    for copy in rests:
-        copy.start()
+            rest_out.at[lax.rem(spot + k, side)],
+            rest_in.at[me],
+            rest_send.at[0],
+            rest_recv.at[0],
+            k,
+        )
     rest_in[me] = rest_out[spot]
 
-    updates = []
     for turn in range(2):
         held = group if turn == 0 else 1 - group
         first = held * side
         for part in range(PARTS):
-            for copy in backs[part][side - 1 :] if turn else backs[part][: side - 1]:
-                copy.wait_recv()
+            await_bytes(
+                back_in.at[pl.ds(0, side - 1 + turn), pl.ds(part * some, some)],
+                back_recv.at[part * 2 + turn],
+            )
             left = jnp.concatenate(
                 [
                     back_in[pl.ds(first, side), owner]
@@ -678,27 +638,21 @@
                     own_update[turn] = made
                 else:
                     update_out[turn, k] = made.astype(bf16)
-                    copy = ray_copy(
+                    ray_copy(
                         update_out.at[turn, k],
                         update_in.at[turn, k],
-                        update_send,
-                        update_recv,
-                        turn * quarters + k,
+                        update_send.at[0],
+                        update_recv.at[turn],
                         ray_twin(k),
                     )
-                    copy.start()
-                    updates.append(copy)
-
-    crossing.wait_recv()
-    relays = [
-        dom_copy(stripe_far.at[spot], stripe_far.at[spot], stripe_send, stripe_recv, k)
-        for k in range(1, side)
-    ]
-    for copy in relays:
-        copy.start()
-
-    for copy in twins:
-        copy.wait_recv()
+
+    await_bytes(stripe_own, stripe_recv.at[0])
+    for k in range(1, side):
+        dom_copy(
+            stripe_far.at[spot], stripe_far.at[spot], stripe_send.at[0], stripe_recv.at[1], k
+        )
+
+    await_bytes(twin_in.at[others], twin_recv.at[0])
     other = pl.ds((1 - group) * side, side)
     own_spots = [carried_ref[me, 0, d] for d in range(owners)]
     taken_by = [twin_in[d].astype(f32) for d in range(owners)]
@@ -707,8 +661,7 @@
         for d in range(owners):
             taken = taken + jnp.where(own_spots[d] == b, 1.0, 0.0).astype(f32) * taken_by[d]
         forward[b] = taken
-    for copy in relays:
-        copy.wait_recv()
+    await_bytes(stripe_far.at[pl.ds(0, side - 1)], stripe_recv.at[1])
     for b in range(count):
         clean = (
             (phase_out[other, (b - 1) % ring].astype(f32) - stripe_far[:, b].astype(f32))
@@ -716,8 +669,7 @@
             .astype(f32)
         )
         rest_in[other, b] = (clean - forward[b]).astype(bf16)
-    for copy in rests:
-        copy.wait_recv()
+    await_bytes(rest_in.at[pl.ds(0, side - 1)], rest_recv.at[0])
     for b in range(count):
         residual_ref[:, b * tile : (b + 1) * tile] = (
             rest_in[:, b].astype(f32).reshape(slices, tile).astype(bf16)
@@ -725,17 +677,23 @@
 
     for turn in range(2):
         held = group if turn == 0 else 1 - group
-        for copy in updates[turn * (quarters - 1) : (turn + 1) * (quarters - 1)]:
-            copy.wait_recv()
+        await_bytes(update_in.at[turn, pl.ds(1, quarters - 1)], update_recv.at[turn])
         amount = own_update[turn]
         for k in range(1, quarters):
             amount = amount + update_in[turn, k].astype(f32)
         rows = pl.ds(pl.multiple_of(held * rows_half, rows_half), rows_half)
         old = image_ref[rows, pl.ds(pl.multiple_of(ray * share, share), share)].astype(f32)
         next_ref[rows, :] = old + relax_factor * amount
-    sent = carries + phases + edges + sum(partials, []) + sum(backs, [])
-    for copy in sent + [crossing] + twins + rests + relays + updates:
-        copy.wait_send()
+    await_bytes(carried_all.at[others], carried_send.at[0])
+    await_bytes(rim, halo_send.at[0])
+    await_bytes(phase_out.at[others, pl.ds(0, inner)], phase_send.at[0])
+    await_bytes(phase_out.at[others, pl.ds(inner, 3)], phase_send.at[1])
+    await_bytes(partial_out.at[others], partial_send.at[0])
+    await_bytes(back_out.at[others], back_send.at[0])
+    await_bytes(twin_in.at[others], twin_send.at[0])
+    await_bytes(rest_out.at[pl.ds(0, side - 1)], rest_send.at[0])
+    await_bytes(stripe_far, stripe_send.at[0])
+    await_bytes(update_out.at[:, pl.ds(1, quarters - 1)], update_send.at[0])
 
 
 def store_kernel(residual_ref, next_ref, residual_out, next_out, sem):
@@ -788,9 +746,7 @@
             pltpu.VMEM((slices, columns), bf16),
             pltpu.VMEM((slices, places * tile), bf16),
             pltpu.VMEM((entries, tile, tile), bf16),
-            pltpu.VMEM((1, capacity), i32),
-            pltpu.VMEM((1, capacity), i32),
-            pltpu.VMEM((1, capacity), i32),
+            pltpu.VMEM((3, 1, capacity), i32),
             pltpu.VMEM((1, owners), i32),
             pltpu.VMEM((owners, 1, owners), i32),
             pltpu.SMEM((owners, 1, owners), i32),
@@ -818,14 +774,26 @@
             pltpu.VMEM((2, rows_half, share), f32),
             pltpu.VMEM((2, quarters, rows_half, share), bf16),
             pltpu.VMEM((2, quarters, rows_half, share), bf16),
-            sems((10,)),
+            sems((7,)),
+            sems((1,)),
+            sems((1,)),
+            sems((1,)),
+            sems((1,)),
             sems((2,)),
             sems((2,)),
-        ]
-        + [sems((owners,))] * 6
-        + [sems((PARTS * owners,))] * 4
-        + [sems((owners,))] * 6
-        + [sems((2 * quarters,))] * 2,
+            sems((1,)),
+            sems((PARTS,)),
+            sems((1,)),
+            sems((2 * PARTS,)),
+            sems((1,)),
+            sems((1,)),
+            sems((1,)),
+            sems((2,)),
+            sems((1,)),
+            sems((1,)),
+            sems((1,)),
+            sems((2,)),
+        ],
         compiler_params=pltpu.CompilerParams(
             collective_id=0, has_side_effects=True, vmem_limit_bytes=48 * 1024 * 1024
         ),

time: 30.4 us -> 28.9 us (0.951)
  Pallas kernels: 28.9 us -> 27.4 us
    pallas_call x1, Pallas kernels: 28.2 us -> 26.6 us  [fast_shards(): pl.pallas_call(functools.partial(step_kernel, owners, quarters), out_shap...]
where the time goes in v4:
time: 28.9 us; the launch traced here: 28.7 us
  Pallas kernels  27.4 us (95%)
  between operations  1.29 us (4%)
    pallas_call x1, Pallas kernels, fast_shards(): pl.pallas_call(functools.partial(step_kernel, owners, quarters), out_shap...  26.6 us
    pallas_call x1, Pallas kernels, fast_shards(): pl.pallas_call(store_kernel, out_shape=(jax.ShapeDtypeStruct(residual.sha...  0.76 us

profile of v4, /device:TPU:0, one launch (start us, length us, event | category | flops | bytes accessed | tf_op | source)
XLA Modules:
  0.0 28.7 jit_solution(1020878431814770647)
XLA Ops:
  1.3 26.6 %shard_map.104 = (bf16[64,2048]{1,0:T(8,128)(2,1)S(1)}, f32[64,512]{1,0:T(8,128)S(1)}) custom-call(bf16[129]{0:T(256)(128)(2,1)} %taps_any.1, bf16[1,64,2048]{2,1,0:T(8,128)(2,1)} %proj_any.1, bf16[64,2048]{1,0:T(8,128)(2,1)} %bitcast.7, bf16[1,1,16,128,128]{4,3,2,1,0:T(8,128)(2,1)} %library_any.1, s32[1,256]{1,0:T(1,128)} %bitcast.8, s32[1,256]{1,0:T(1,128)} %bitcast.9, ...), custom_call_target="tpu_custom_call" | custom-call | tf_op jit(solution)/shard_map/pallas_call | solution.py:736
  27.9 0.8 %shard_map.105 = (bf16[64,2048]{1,0:T(8,128)(2,1)}, f32[64,512]{1,0:T(8,128)}) custom-call(bf16[64,2048]{1,0:T(8,128)(2,1)S(1)} %get-tuple-element.6.residual_ref, f32[64,512]{1,0:T(8,128)S(1)} %get-tuple-element.7.next_ref), custom_call_target="tpu_custom_call" | custom-call | tf_op jit(solution)/shard_map/pallas_call | solution.py:816

commit v5 on v4

--- a/solution.py
+++ b/solution.py
@@ -165,7 +165,7 @@
 NT = (((1,), (1,)), ((), ()))
 NN = (((1,), (0,)), ((), ()))
 SUB = 16
-PARTS = 2
+PARTS = 4
 
 
 def dot(a, b, dims):
@@ -472,14 +472,7 @@
         )
     phase_in[me] = phase_out[me]
 
-    await_bytes(image_ref, load_sem.at[5])
-    for part in range(PARTS):
-        for owner in range(part * some, (part + 1) * some, 2):
-            made = dot(image_ref[...], matrix[owner * tile : (owner + 2) * tile, :], NT)
-            for i in range(2):
-                partial_out[:, owner + i] = (
-                    made[:, i * tile : (i + 1) * tile].reshape(owners, per, tile).astype(bf16)
-                )
+    def send_partials(part):
         chosen = pl.ds(part * some, some)
         for k in dom_order:
             dom_copy(
@@ -489,7 +482,33 @@
                 partial_recv.at[part],
                 k,
             )
+
+    def send_all_partials():
+        for part in range(PARTS):
+            send_partials(part)
+
+    await_bytes(image_ref, load_sem.at[5])
+    for part in range(PARTS):
+        for owner in range(part * some, (part + 1) * some, 2):
+            made = dot(image_ref[...], matrix[owner * tile : (owner + 2) * tile, :], NT)
+            for i in range(2):
+                partial_out[:, owner + i] = (
+                    made[:, i * tile : (i + 1) * tile].reshape(owners, per, tile).astype(bf16)
+                )
+        pl.when(core == 0)(functools.partial(send_partials, part))
     partial_in[me] = partial_out[me]
+
+    def send_twins():
+        for k in dom_order:
+            dom_copy(
+                partial_out.at[pl.ds((1 - dom_peer(k) // side) * side, side), dom_peer(k)],
+                twin_in.at[me],
+                twin_send.at[0],
+                twin_recv.at[0],
+                k,
+            )
+
+    twin_in[me] = partial_out[pl.ds((1 - group) * side, side), me]
 
     carried_all[me] = carried_own[...]
     await_bytes(carried_all.at[pl.ds(0, owners - 1)], carried_recv.at[0])
@@ -514,6 +533,7 @@
     for i in range(inner):
         profile_ref[:, i * tile : (i + 1) * tile] = profile_of(i)
     await_bytes(phase_in.at[others, pl.ds(inner, 3)], phase_recv.at[1])
+    pl.when(core == 1)(send_all_partials)
     for i in range(inner, ring):
         profile_ref[:, i * tile : (i + 1) * tile] = profile_of(i)
 
@@ -574,17 +594,6 @@
             )
     back_in[me] = back_out[me]
 
-    dom_copy(stripe_own, stripe_far.at[spot], stripe_send.at[0], stripe_recv.at[0], side)
-    for k in dom_order:
-        dom_copy(
-            partial_out.at[pl.ds((1 - dom_peer(k) // side) * side, side), dom_peer(k)],
-            twin_in.at[me],
-            twin_send.at[0],
-            twin_recv.at[0],
-            k,
-        )
-    twin_in[me] = partial_out[pl.ds((1 - group) * side, side), me]
-
     def whole(i, carry):
         owner = group * side + i
         part = [partial_in[d, owner].astype(f32) for d in range(owners)]
@@ -598,59 +607,81 @@
         return carry
 
     lax.fori_loop(0, side, whole, 0)
-    for k in range(1, side):
-        dom_copy(
-            rest_out.at[lax.rem(spot + k, side)],
-            rest_in.at[me],
-            rest_send.at[0],
-            rest_recv.at[0],
-            k,
-        )
+    dom_copy(stripe_own, stripe_far.at[spot], stripe_send.at[0], stripe_recv.at[0], side)
     rest_in[me] = rest_out[spot]
 
+    def rows_of(turn, part):
+        first = (group if turn == 0 else 1 - group) * side
+        return jnp.concatenate(
+            [
+                back_in[pl.ds(first, side), owner]
+                .astype(f32)
+                .reshape(rows_half, tile)
+                .astype(bf16)
+                for owner in range(part * some, (part + 1) * some)
+            ],
+            axis=1,
+        )
+
+    def send_update(turn, k, sem):
+        ray_copy(
+            update_out.at[turn, k],
+            update_in.at[turn, k],
+            update_send.at[0],
+            update_recv.at[sem],
+            ray_twin(k),
+        )
+
     for turn in range(2):
-        held = group if turn == 0 else 1 - group
-        first = held * side
         for part in range(PARTS):
             await_bytes(
                 back_in.at[pl.ds(0, side - 1 + turn), pl.ds(part * some, some)],
                 back_recv.at[part * 2 + turn],
             )
-            left = jnp.concatenate(
-                [
-                    back_in[pl.ds(first, side), owner]
-                    .astype(f32)
-                    .reshape(rows_half, tile)
-                    .astype(bf16)
-                    for owner in range(part * some, (part + 1) * some)
-                ],
-                axis=1,
-            )
+            left = rows_of(turn, part)
             rows = slice(part * some * tile, (part + 1) * some * tile)
-            for k in (2, 3, 1, 0):
+            for k in (2, 3):
                 start = pl.multiple_of(ray_twin(k) * share, share)
                 made = dot(left, matrix[rows, pl.ds(start, share)], NN)
                 if part > 0:
-                    made = made + gathered[k]
+                    made = made + gathered[k - 2]
                 if part < PARTS - 1:
-                    gathered[k] = made
-                elif k == 0:
-                    own_update[turn] = made
+                    gathered[k - 2] = made
                 else:
                     update_out[turn, k] = made.astype(bf16)
-                    ray_copy(
-                        update_out.at[turn, k],
-                        update_in.at[turn, k],
-                        update_send.at[0],
-                        update_recv.at[turn],
-                        ray_twin(k),
-                    )
+                    send_update(turn, k, turn)
+        if turn == 0:
+            send_twins()
+            for k in range(1, side):
+                dom_copy(
+                    rest_out.at[lax.rem(spot + k, side)],
+                    rest_in.at[me],
+                    rest_send.at[0],
+                    rest_recv.at[0],
+                    k,
+                )
+
+    left = jnp.concatenate(
+        [
+            jnp.concatenate([rows_of(turn, part) for part in range(PARTS)], axis=1)
+            for turn in range(2)
+        ],
+        axis=0,
+    )
+    start = pl.multiple_of(ray_twin(1) * share, share)
+    made = dot(left, matrix[:, pl.ds(start, share)], NN).reshape(2, rows_half, share)
+    update_out[:, 1] = made.astype(bf16)
+    for turn in range(2):
+        send_update(turn, 1, 2)
 
     await_bytes(stripe_own, stripe_recv.at[0])
     for k in range(1, side):
         dom_copy(
             stripe_far.at[spot], stripe_far.at[spot], stripe_send.at[0], stripe_recv.at[1], k
         )
+
+    start = pl.multiple_of(ray * share, share)
+    own_update[...] = dot(left, matrix[:, pl.ds(start, share)], NN).reshape(2, rows_half, share)
 
     await_bytes(twin_in.at[others], twin_recv.at[0])
     other = pl.ds((1 - group) * side, side)
@@ -675,9 +706,10 @@
             rest_in[:, b].astype(f32).reshape(slices, tile).astype(bf16)
         )
 
+    await_bytes(update_in.at[:, 1], update_recv.at[2])
     for turn in range(2):
         held = group if turn == 0 else 1 - group
-        await_bytes(update_in.at[turn, pl.ds(1, quarters - 1)], update_recv.at[turn])
+        await_bytes(update_in.at[turn, pl.ds(2, quarters - 2)], update_recv.at[turn])
         amount = own_update[turn]
         for k in range(1, quarters):
             amount = amount + update_in[turn, k].astype(f32)
@@ -770,7 +802,7 @@
             pltpu.VMEM((owners // 2, count, per, tile), bf16),
             pltpu.VMEM((owners, owners // 2, per, tile), bf16),
             pltpu.VMEM((count, owners // 2, per, tile), f32),
-            pltpu.VMEM((quarters, rows_half, share), f32),
+            pltpu.VMEM((2, rows_half, share), f32),
             pltpu.VMEM((2, rows_half, share), f32),
             pltpu.VMEM((2, quarters, rows_half, share), bf16),
             pltpu.VMEM((2, quarters, rows_half, share), bf16),
@@ -792,7 +824,7 @@
             sems((1,)),
             sems((1,)),
             sems((1,)),
-            sems((2,)),
+            sems((3,)),
         ],
         compiler_params=pltpu.CompilerParams(
             collective_id=0, has_side_effects=True, vmem_limit_bytes=48 * 1024 * 1024

time: 28.9 us -> 27.5 us (0.952)
  Pallas kernels: 27.4 us -> 26 us
    pallas_call x1, Pallas kernels: 26.6 us -> 25.2 us  [fast_shards(): pl.pallas_call(functools.partial(step_kernel, owners, quarters), out_shap...]
where the time goes in v5:
time: 27.5 us; the launch traced here: 27.3 us
  Pallas kernels  26 us (95%)
  between operations  1.29 us (5%)
    pallas_call x1, Pallas kernels, fast_shards(): pl.pallas_call(functools.partial(step_kernel, owners, quarters), out_shap...  25.2 us
    pallas_call x1, Pallas kernels, fast_shards(): pl.pallas_call(store_kernel, out_shape=(jax.ShapeDtypeStruct(residual.sha...  0.76 us

profile of v5, /device:TPU:0, one launch (start us, length us, event | category | flops | bytes accessed | tf_op | source)
XLA Modules:
  0.0 27.3 jit_solution(9442138064912966687)
XLA Ops:
  1.3 25.2 %shard_map.104 = (bf16[64,2048]{1,0:T(8,128)(2,1)S(1)}, f32[64,512]{1,0:T(8,128)S(1)}) custom-call(bf16[129]{0:T(256)(128)(2,1)} %taps_any.1, bf16[1,64,2048]{2,1,0:T(8,128)(2,1)} %proj_any.1, bf16[64,2048]{1,0:T(8,128)(2,1)} %bitcast.7, bf16[1,1,16,128,128]{4,3,2,1,0:T(8,128)(2,1)} %library_any.1, s32[1,256]{1,0:T(1,128)} %bitcast.8, s32[1,256]{1,0:T(1,128)} %bitcast.9, ...), custom_call_target="tpu_custom_call" | custom-call | tf_op jit(solution)/shard_map/pallas_call | solution.py:768
  26.5 0.8 %shard_map.105 = (bf16[64,2048]{1,0:T(8,128)(2,1)}, f32[64,512]{1,0:T(8,128)}) custom-call(bf16[64,2048]{1,0:T(8,128)(2,1)S(1)} %get-tuple-element.6.residual_ref, f32[64,512]{1,0:T(8,128)S(1)} %get-tuple-element.7.next_ref), custom_call_target="tpu_custom_call" | custom-call | tf_op jit(solution)/shard_map/pallas_call | solution.py:848

commit v6 on v5

--- a/solution.py
+++ b/solution.py
@@ -608,6 +608,14 @@
 
     lax.fori_loop(0, side, whole, 0)
     dom_copy(stripe_own, stripe_far.at[spot], stripe_send.at[0], stripe_recv.at[0], side)
+    for k in range(1, side):
+        dom_copy(
+            rest_out.at[lax.rem(spot + k, side)],
+            rest_in.at[me],
+            rest_send.at[0],
+            rest_recv.at[0],
+            k,
+        )
     rest_in[me] = rest_out[spot]
 
     def rows_of(turn, part):
@@ -652,14 +660,6 @@
                     send_update(turn, k, turn)
         if turn == 0:
             send_twins()
-            for k in range(1, side):
-                dom_copy(
-                    rest_out.at[lax.rem(spot + k, side)],
-                    rest_in.at[me],
-                    rest_send.at[0],
-                    rest_recv.at[0],
-                    k,
-                )
 
     left = jnp.concatenate(
         [

time: 27.5 us -> 27.3 us (level)
  no operation moved by 1% of the time
where the time goes in v6:
time: 27.3 us; the launch traced here: 27.1 us
  Pallas kernels  25.8 us (95%)
  between operations  1.29 us (5%)
    pallas_call x1, Pallas kernels, fast_shards(): pl.pallas_call(functools.partial(step_kernel, owners, quarters), out_shap...  25.1 us
    pallas_call x1, Pallas kernels, fast_shards(): pl.pallas_call(store_kernel, out_shape=(jax.ShapeDtypeStruct(residual.sha...  0.76 us

profile of v6, /device:TPU:0, one launch (start us, length us, event | category | flops | bytes accessed | tf_op | source)
XLA Modules:
  0.0 27.1 jit_solution(16539158035956680378)
XLA Ops:
  1.3 25.1 %shard_map.104 = (bf16[64,2048]{1,0:T(8,128)(2,1)S(1)}, f32[64,512]{1,0:T(8,128)S(1)}) custom-call(bf16[129]{0:T(256)(128)(2,1)} %taps_any.1, bf16[1,64,2048]{2,1,0:T(8,128)(2,1)} %proj_any.1, bf16[64,2048]{1,0:T(8,128)(2,1)} %bitcast.7, bf16[1,1,16,128,128]{4,3,2,1,0:T(8,128)(2,1)} %library_any.1, s32[1,256]{1,0:T(1,128)} %bitcast.8, s32[1,256]{1,0:T(1,128)} %bitcast.9, ...), custom_call_target="tpu_custom_call" | custom-call | tf_op jit(solution)/shard_map/pallas_call | solution.py:768
  26.4 0.8 %shard_map.105 = (bf16[64,2048]{1,0:T(8,128)(2,1)}, f32[64,512]{1,0:T(8,128)}) custom-call(bf16[64,2048]{1,0:T(8,128)(2,1)S(1)} %get-tuple-element.6.residual_ref, f32[64,512]{1,0:T(8,128)S(1)} %get-tuple-element.7.next_ref), custom_call_target="tpu_custom_call" | custom-call | tf_op jit(solution)/shard_map/pallas_call | solution.py:848

commit v7 on v6

--- a/solution.py
+++ b/solution.py
@@ -284,6 +284,7 @@
         return group * side + lax.rem(spot + k, side)
 
     dom_order = list(range(1, owners))
+    far_order = list(range(side, owners)) + list(range(1, side))
 
     chip, core = ray // 2, lax.rem(ray, 2)
 
@@ -374,7 +375,7 @@
         halo_recv.at[0],
         ray_next(quarters - 1),
     )
-    for k in dom_order:
+    for k in far_order:
         dom_copy(
             phase_out.at[dom_peer(k), pl.ds(0, inner)],
             phase_in.at[me, pl.ds(0, inner)],
@@ -462,7 +463,7 @@
     phase_out[:, inner] = edge[0].astype(bf16)
     phase_out[:, inner + 1] = jnp.where(lane < half, edge[1], edge[3]).astype(bf16)
     phase_out[:, inner + 2] = edge[2].astype(bf16)
-    for k in dom_order:
+    for k in far_order:
         dom_copy(
             phase_out.at[dom_peer(k), pl.ds(inner, 3)],
             phase_in.at[me, pl.ds(inner, 3)],
@@ -474,7 +475,7 @@
 
     def send_partials(part):
         chosen = pl.ds(part * some, some)
-        for k in dom_order:
+        for k in far_order:
             dom_copy(
                 partial_out.at[dom_peer(k), chosen],
                 partial_in.at[me, chosen],
@@ -729,14 +730,14 @@
 
 
 def store_kernel(residual_ref, next_ref, residual_out, next_out, sem):
-    copies = [
-        pltpu.make_async_copy(residual_ref, residual_out, sem.at[0]),
-        pltpu.make_async_copy(next_ref, next_out, sem.at[1]),
-    ]
-    for copy in copies:
-        copy.start()
-    for copy in copies:
-        copy.wait()
+    pairs = [(residual_ref, residual_out), (next_ref, next_out)]
+    for i, (src, dst) in enumerate(pairs):
+        rows = src.shape[0] // 2
+        for part in range(2):
+            piece = pl.ds(part * rows, rows)
+            pltpu.make_async_copy(src.at[piece], dst.at[piece], sem.at[i]).start()
+    for i, (src, dst) in enumerate(pairs):
+        pltpu.make_async_copy(src, dst, sem.at[i]).wait()
 
 
 def fast_shards(

time: 27.3 us -> 27.1 us (level)
  no operation moved by 1% of the time
where the time goes in v7:
time: 27.1 us; the launch traced here: 26.9 us
  Pallas kernels  25.6 us (94%)
  between operations  1.29 us (5%)
    pallas_call x1, Pallas kernels, fast_shards(): pl.pallas_call(functools.partial(step_kernel, owners, quarters), out_shap...  24.9 us
    pallas_call x1, Pallas kernels, fast_shards(): pl.pallas_call(store_kernel, out_shape=(jax.ShapeDtypeStruct(residual.sha...  0.76 us

profile of v7, /device:TPU:0, one launch (start us, length us, event | category | flops | bytes accessed | tf_op | source)
XLA Modules:
  0.0 26.9 jit_solution(13641400994675352419)
XLA Ops:
  1.3 24.9 %shard_map.104 = (bf16[64,2048]{1,0:T(8,128)(2,1)S(1)}, f32[64,512]{1,0:T(8,128)S(1)}) custom-call(bf16[129]{0:T(256)(128)(2,1)} %taps_any.1, bf16[1,64,2048]{2,1,0:T(8,128)(2,1)} %proj_any.1, bf16[64,2048]{1,0:T(8,128)(2,1)} %bitcast.7, bf16[1,1,16,128,128]{4,3,2,1,0:T(8,128)(2,1)} %library_any.1, s32[1,256]{1,0:T(1,128)} %bitcast.8, s32[1,256]{1,0:T(1,128)} %bitcast.9, ...), custom_call_target="tpu_custom_call" | custom-call | tf_op jit(solution)/shard_map/pallas_call | solution.py:769
  26.2 0.8 %shard_map.105 = (bf16[64,2048]{1,0:T(8,128)(2,1)}, f32[64,512]{1,0:T(8,128)}) custom-call(bf16[64,2048]{1,0:T(8,128)(2,1)S(1)} %get-tuple-element.6.residual_ref, f32[64,512]{1,0:T(8,128)S(1)} %get-tuple-element.7.next_ref), custom_call_target="tpu_custom_call" | custom-call | tf_op jit(solution)/shard_map/pallas_call | solution.py:849

commit v8 on v7

--- a/solution.py
+++ b/solution.py
@@ -473,9 +473,9 @@
         )
     phase_in[me] = phase_out[me]
 
-    def send_partials(part):
+    def send_partials(part, order):
         chosen = pl.ds(part * some, some)
-        for k in far_order:
+        for k in order:
             dom_copy(
                 partial_out.at[dom_peer(k), chosen],
                 partial_in.at[me, chosen],
@@ -486,7 +486,7 @@
 
     def send_all_partials():
         for part in range(PARTS):
-            send_partials(part)
+            send_partials(part, far_order[:side])
 
     await_bytes(image_ref, load_sem.at[5])
     for part in range(PARTS):
@@ -496,7 +496,8 @@
                 partial_out[:, owner + i] = (
                     made[:, i * tile : (i + 1) * tile].reshape(owners, per, tile).astype(bf16)
                 )
-        pl.when(core == 0)(functools.partial(send_partials, part))
+        pl.when(core == 0)(functools.partial(send_partials, part, far_order[:side]))
+        send_partials(part, far_order[side:])
     partial_in[me] = partial_out[me]
 
     def send_twins():
@@ -607,8 +608,8 @@
             rest_out[i, b] = (total - taken).astype(bf16)
         return carry
 
+    dom_copy(stripe_own, stripe_far.at[spot], stripe_send.at[0], stripe_recv.at[0], side)
     lax.fori_loop(0, side, whole, 0)
-    dom_copy(stripe_own, stripe_far.at[spot], stripe_send.at[0], stripe_recv.at[0], side)
     for k in range(1, side):
         dom_copy(
             rest_out.at[lax.rem(spot + k, side)],

time: 27.1 us -> 27.1 us (level)
  no operation moved by 1% of the time
where the time goes in v8:
time: 27.1 us; the launch traced here: 26.9 us
  Pallas kernels  25.6 us (94%)
  between operations  1.29 us (5%)
    pallas_call x1, Pallas kernels, fast_shards(): pl.pallas_call(functools.partial(step_kernel, owners, quarters), out_shap...  24.9 us
    pallas_call x1, Pallas kernels, fast_shards(): pl.pallas_call(store_kernel, out_shape=(jax.ShapeDtypeStruct(residual.sha...  0.76 us

profile of v8, /device:TPU:0, one launch (start us, length us, event | category | flops | bytes accessed | tf_op | source)
XLA Modules:
  0.0 26.9 jit_solution(3313135406281820495)
XLA Ops:
  1.3 24.9 %shard_map.104 = (bf16[64,2048]{1,0:T(8,128)(2,1)S(1)}, f32[64,512]{1,0:T(8,128)S(1)}) custom-call(bf16[129]{0:T(256)(128)(2,1)} %taps_any.1, bf16[1,64,2048]{2,1,0:T(8,128)(2,1)} %proj_any.1, bf16[64,2048]{1,0:T(8,128)(2,1)} %bitcast.7, bf16[1,1,16,128,128]{4,3,2,1,0:T(8,128)(2,1)} %library_any.1, s32[1,256]{1,0:T(1,128)} %bitcast.8, s32[1,256]{1,0:T(1,128)} %bitcast.9, ...), custom_call_target="tpu_custom_call" | custom-call | tf_op jit(solution)/shard_map/pallas_call | solution.py:770
  26.2 0.8 %shard_map.105 = (bf16[64,2048]{1,0:T(8,128)(2,1)}, f32[64,512]{1,0:T(8,128)}) custom-call(bf16[64,2048]{1,0:T(8,128)(2,1)S(1)} %get-tuple-element.6.residual_ref, f32[64,512]{1,0:T(8,128)S(1)} %get-tuple-element.7.next_ref), custom_call_target="tpu_custom_call" | custom-call | tf_op jit(solution)/shard_map/pallas_call | solution.py:850
